TPU v7x, 512 devices: a 8x2x16 block of a 8x8x16 slice. The times are simulated.
512 devices in a mesh: group: 2 (over y), dev: 128 (over x, z), tp: 2 (over core).
Axes of the slice: x: 8, y: 2, z: 16, core: 2. Of those that a mesh axis runs over, the one named last changes fastest.
The devices are a block of a 8x8x16 slice.
Arguments:
- prompt_activations: bfloat16 [65536, 8192], P(('group', 'dev')), parts along dimension 0, may hold values from -6 to 6
- key_matrix: bfloat16 [8192, 512], P('dev', 'tp'), may hold values from -0.0625 to 0.0625
- value_matrix: bfloat16 [8192, 512], P('dev', 'tp'), may hold values from -0.0625 to 0.0625
- adapter_down_keyvalue: bfloat16 [8192, 128], P('dev'), may hold values from -0.0625 to 0.0625
- adapter_up_key: bfloat16 [64, 512], P(None, 'tp'), may hold values from -1.5 to 1.5
- adapter_up_value: bfloat16 [64, 512], P(None, 'tp'), may hold values from -1.5 to 1.5
- request_adapter: int32 [256], P('group'), parts along dimension 0, may hold values from 0 to 3
- page_request: int32 [16384, 1], P('group'), parts along dimension 0, may hold values from 0 to 127; in each aligned block of 64 rows (0 to 63, 64 to 127, ...) at most 2 rows name the same one
- context_tokens: int32 [256], P('group'), parts along dimension 0, may hold values from 64 to 256
- step_query: bfloat16 [256, 4096], P(('group', 'dev'), 'tp'), parts along dimension 0, may hold values from -256 to 256
- step_key: bfloat16 [256, 512], P(('group', 'dev'), 'tp'), parts along dimension 0, may hold values from -6 to 6
- step_value: bfloat16 [256, 512], P(('group', 'dev'), 'tp'), parts along dimension 0, may hold values from -6 to 6
- stored_keys: bfloat16 [256, 256, 512], P(('group', 'dev'), None, 'tp'), parts along dimension 0, may hold values from -6 to 6
- stored_values: bfloat16 [256, 256, 512], P(('group', 'dev'), None, 'tp'), parts along dimension 0, may hold values from -6 to 6
- output_matrix: bfloat16 [4096, 8192], P('tp', 'dev'), may hold values from -0.09375 to 0.09375
- adapter_down_output: bfloat16 [4096, 64], P('tp'), may hold values from -0.09375 to 0.09375
- adapter_up_output: bfloat16 [64, 8192], P(None, 'dev'), may hold values from -1.5 to 1.5
Outputs:
- attended: bfloat16 [256, 8192], P('group', 'dev'), parts along dimension 0
There are 2 independent parts, one for each index of `group`. A program takes and returns all parts, laid end to end along the dimension named above; an argument that names none is the same for every part. Nothing has to cross between parts.
Inputs may be any that keep to these rules, and one draw needn't show every extreme that they name: `page_request`: among the pages of one device's prompt block (aligned blocks of 64 pages), no request owns more than 2; every request owns at least one page.
All inputs are finite; a program needn't handle non-finite values.
Results may differ from a plain program's by a relative error of at most 0.0086.
Values may be sent and summed in bfloat16 or wider, within the bound.
No kernel may reach another device: no remote copies, remote signals or barrier semaphores. Data moves between devices by JAX's collectives and lax.ppermute only.
A program may use at most 64 MiB of HBM per device.

v0:
```python
import functools

import jax
import jax.numpy as jnp
from jax import lax
from jax.experimental import pallas as pl
from jax.experimental.pallas import tpu as pltpu
from jax.sharding import Mesh
from jax.sharding import PartitionSpec as P


HEADS = 32
KV_HEADS = 4
HEAD = 128
LOW_RANK = 16
ADAPTER_COUNT = 4
PAGE = 4
LORA = ADAPTER_COUNT * LOW_RANK
DEV = ("x", "zh", "zm", "zp")
GROUP_DEV = ("group", "x", "zh", "zm", "zp")
Z8 = ("zh", "zm")
NEAR = ("x", "zm", "zp")
NX, NZH, NZM, NZP = 8, 4, 2, 2
NEG = -1e30

rope_base = 500000.0


f32 = jnp.float32
bf16 = jnp.bfloat16
SMEM = pl.BlockSpec(memory_space=pltpu.SMEM)
VMEM = pl.BlockSpec(memory_space=pltpu.VMEM)


def ring_x(x, step):
    return lax.ppermute(x, "x", [(i, (i + step) % NX) for i in range(NX)])


def swap_pair(x):
    return lax.ppermute(x, "zp", [(0, 1), (1, 0)])


def split_kernel(p_ref, a_ref, mine_ref, other_ref):
    parity = p_ref[0]
    half = HEAD // 2
    lane = lax.broadcasted_iota(jnp.int32, (a_ref.shape[0], HEAD), 1)
    low = lane < half
    first = parity == 0
    for k in range(mine_ref.shape[1] // HEAD):
        t0 = a_ref[:, 2 * k * HEAD : (2 * k + 1) * HEAD].astype(f32)
        t1 = a_ref[:, (2 * k + 1) * HEAD : (2 * k + 2) * HEAD].astype(f32)
        even = jnp.where(low, t0, pltpu.roll(t1, half, 1))
        odd = jnp.where(low, pltpu.roll(t0, half, 1), t1)
        cols = slice(k * HEAD, (k + 1) * HEAD)
        mine_ref[:, cols] = jnp.where(first, even, odd).astype(bf16)
        other_ref[:, cols] = jnp.where(first, odd, even).astype(bf16)


def split_columns(act, parity):
    rows, width = act.shape
    block = 64
    out = jax.ShapeDtypeStruct((rows, width // 2), bf16)
    return pl.pallas_call(
        split_kernel,
        grid=(rows // block,),
        in_specs=[SMEM, pl.BlockSpec((block, width), lambda i: (i, 0))],
        out_specs=[pl.BlockSpec((block, width // 2), lambda i: (i, 0))] * 2,
        out_shape=[out, out],
        name="split_columns",
    )(parity, act)


def project_kernel(offsets, chunks, depth, x_ref, a_ref, *refs):
    count = len(offsets) * chunks
    pieces, out_ref = refs[:count], refs[count]
    a_buf, w_buf, a_sem, w_sem = refs[count + 1 :]
    load_a = pltpu.make_async_copy(a_ref, a_buf, a_sem)
    load_a.start()
    loads = []
    for j in range(count):
        load = pltpu.make_async_copy(pieces[j].at[pl.ds(0, depth)], w_buf.at[j], w_sem.at[j])
        load.start()
        loads.append(load)
    me = x_ref[0]
    load_a.wait()
    total = jnp.zeros(out_ref.shape, f32)
    for i, off in enumerate(offsets):
        where = lax.rem(me + off, NX)
        for c in range(chunks):
            start = pl.multiple_of((where * chunks + c) * depth, depth)
            loads[i * chunks + c].wait()
            a = a_buf[:, pl.ds(start, depth)]
            total = total + jnp.dot(a, w_buf[i * chunks + c], preferred_element_type=f32)
    out_ref[...] = total.astype(out_ref.dtype)


def project(act, offsets, pieces, depth, me, dtype):
    chunks = len(pieces) // len(offsets)
    width = pieces[0].shape[1]
    anywhere = pl.BlockSpec(memory_space=pl.ANY)
    return pl.pallas_call(
        functools.partial(project_kernel, offsets, chunks, depth),
        in_specs=[SMEM] + [anywhere] * (1 + len(pieces)),
        out_specs=VMEM,
        out_shape=jax.ShapeDtypeStruct((act.shape[0], width), dtype),
        scratch_shapes=[
            pltpu.VMEM(act.shape, bf16),
            pltpu.VMEM((len(pieces), depth, width), bf16),
            pltpu.SemaphoreType.DMA,
            pltpu.SemaphoreType.DMA((len(pieces),)),
        ],
        name="project",
    )(me, act, *pieces)


def collect_kernel(*refs):
    out_ref = refs[-1]
    rows, width = refs[0].shape[0], out_ref.shape[1]
    for j, ref in enumerate(refs[:-1]):
        out_ref[j * rows : (j + 1) * rows, :] = ref[:, :width]


def collect_tails(pieces, depth, width):
    rows = pieces[0].shape[0] - depth
    tail = pl.BlockSpec((rows, pieces[0].shape[1]), lambda i: (depth // rows, 0))
    total = rows * len(pieces)
    return pl.pallas_call(
        collect_kernel,
        grid=(1,),
        in_specs=[tail] * len(pieces),
        out_specs=pl.BlockSpec((total, width), lambda i: (0, 0)),
        out_shape=jax.ShapeDtypeStruct((total, width), bf16),
        name="collect_tails",
    )(*pieces)


def two_terms(v):
    hi = v.astype(bf16)
    return hi, (v - hi.astype(f32)).astype(bf16)


def dot_fine(v, w):
    hi, lo = two_terms(v)
    return jnp.dot(hi, w, preferred_element_type=f32) + jnp.dot(lo, w, preferred_element_type=f32)


def three_terms(v):
    hi = v.astype(bf16).astype(f32)
    mid = (v - hi).astype(bf16).astype(f32)
    return hi, mid, v - hi - mid


def partial_kernel(
    heads, kv, s_ref, base_ref, other_ref, upk_ref, upv_ref, cos_ref, sin_ref,
    adapter_ref, owner_ref, q0_ref, q1_ref, out_ref,
):
    me, parity = s_ref[0], s_ref[1]
    tokens = base_ref.shape[0]
    rows = out_ref.shape[0]
    width = kv * HEAD
    raw = base_ref[...] + other_ref[...].astype(f32)
    column = lax.broadcasted_iota(jnp.int32, (tokens, 2 * LORA), 1)
    kept = lax.rem(column, LORA) // LOW_RANK == adapter_ref[...]
    chosen = jnp.where(kept, raw[:, 2 * width :], 0.0)
    key = raw[:, :width] + dot_fine(chosen[:, :LORA], upk_ref[...])
    value = (raw[:, width : 2 * width] + dot_fine(chosen[:, LORA:], upv_ref[...])).astype(bf16)
    turned = []
    for k in range(kv):
        part = key[:, k * HEAD : (k + 1) * HEAD]
        spun = part * cos_ref[...] + pltpu.roll(part, HEAD // 2, 1) * sin_ref[...]
        turned.append(spun.astype(bf16))
    source = q0_ref.shape[0]
    blocks = 4
    i = lax.broadcasted_iota(jnp.int32, (rows, source), 1)
    row = lax.broadcasted_iota(jnp.int32, (rows, source), 0)
    row_half = lax.rem(row // NZH, 2)
    row_base = row - row_half * NZH
    block = lax.rem(i, blocks)
    z8 = lax.rem(i // blocks, NZH * NZM)
    off = i // (blocks * NZH * NZM)
    xs = lax.rem(off + me, NX)
    spot = (xs * (NZM * NZP) + lax.rem(z8, NZM) * NZP) * (2 * NZH) + z8 // NZM
    hit0 = row_base == spot + parity * (2 * NZH)
    hit1 = row_base == spot + (1 - parity) * (2 * NZH)
    queries = []
    for g in range(2):
        right = block == 2 * row_half + g
        pick0 = jnp.where(hit0 & right, 1.0, 0.0).astype(bf16)
        pick1 = jnp.where(hit1 & right, 1.0, 0.0).astype(bf16)
        got = jnp.dot(pick0, q0_ref[...], preferred_element_type=f32) + jnp.dot(
            pick1, q1_ref[...], preferred_element_type=f32
        )
        queries.append(got.astype(bf16))
    t_row = lax.broadcasted_iota(jnp.int32, (rows, tokens), 0)
    t_first = lax.rem(t_row // NZH, 2) == 0
    mask = t_row - jnp.where(t_first, 0, NZH) == owner_ref[...]
    lane = lax.broadcasted_iota(jnp.int32, (rows, HEAD), 1)
    stat = jnp.zeros((rows, HEAD), f32)
    across = (((1,), (1,)), ((), ()))
    for h in range(heads):
        q = queries[h // 4][:, (h % 4) * HEAD : (h % 4 + 1) * HEAD]
        s0 = lax.dot_general(q, turned[0], across, preferred_element_type=f32)
        s1 = lax.dot_general(q, turned[1], across, preferred_element_type=f32)
        s = jnp.where(mask, jnp.where(t_first, s0, s1) * (HEAD ** (-0.5)), NEG)
        top = jnp.max(s, axis=1, keepdims=True)
        e = jnp.where(mask, jnp.exp(s - top), 0.0)
        total = jnp.sum(e, axis=1, keepdims=True)
        e0 = jnp.where(t_first, e, 0.0).astype(bf16)
        e1 = jnp.where(t_first, 0.0, e).astype(bf16)
        o = jnp.dot(e0, value[:, :HEAD], preferred_element_type=f32) + jnp.dot(
            e1, value[:, HEAD:], preferred_element_type=f32
        )
        full = total > 0.0
        o = o * jnp.where(full, 1.0 / jnp.maximum(total, 1e-30), 0.0)
        out_ref[:, h * HEAD : (h + 1) * HEAD] = o.astype(bf16)
        lse = jnp.where(full, top + jnp.log(jnp.maximum(total, 1e-30)), NEG)
        hi, mid, lo = three_terms(lse)
        stat = jnp.where(lane == h, hi, stat)
        stat = jnp.where(lane == heads + h, mid, stat)
        stat = jnp.where(lane == 2 * heads + h, lo, stat)
    out_ref[:, heads * HEAD :] = stat.astype(bf16)


def reduce_rows(v, op):
    while v.shape[0] > 8:
        half = v.shape[0] // 2
        v = op(v[:half], v[half:])
    return v


def merge(heads, x_ref, cached, out_ref, with_stat):
    rows = x_ref.shape[0]
    copies = out_ref.shape[0] // 8
    st = x_ref[:, heads * HEAD :].astype(f32)
    lse = st + pltpu.roll(st, HEAD - heads, 1) + pltpu.roll(st, HEAD - 2 * heads, 1)
    lane = lax.broadcasted_iota(jnp.int32, (rows, HEAD), 1)
    lse = jnp.where(lane < heads, lse, 0.0)
    top = reduce_rows(lse, jnp.maximum)
    if cached is not None:
        zh, o_ref, lse_ref = cached
        row = lax.broadcasted_iota(jnp.int32, (8, HEAD), 0)
        first = row < NZH
        here = lax.rem(row, NZH) == zh
        cache_lse = jnp.where(first, lse_ref[0:1, :], lse_ref[1:2, :])
        top = jnp.where(here, jnp.maximum(top, cache_lse), top)
        cache_w = jnp.where(here, jnp.exp(cache_lse - top), 0.0)
    w = jnp.exp(lse - jnp.tile(top, (rows // 8, 1)))
    total = reduce_rows(w, jnp.add)
    if cached is not None:
        total = total + cache_w
    for h in range(heads):
        cols = slice(h * HEAD, (h + 1) * HEAD)
        o = reduce_rows(w[:, h : h + 1] * x_ref[:, cols].astype(f32), jnp.add)
        if cached is not None:
            kept = jnp.where(first, o_ref[0:1, cols], o_ref[1:2, cols])
            o = o + cache_w[:, h : h + 1] * kept
        o = (o / total[:, h : h + 1]).astype(bf16)
        for c in range(copies):
            out_ref[c * 8 : (c + 1) * 8, cols] = o
    if with_stat:
        final = top + jnp.log(total)
        hi, mid, lo = three_terms(jnp.where(lane[:8] < heads, final, 0.0))
        stat = hi + pltpu.roll(mid, heads, 1) + pltpu.roll(lo, 2 * heads, 1)
        for c in range(copies):
            out_ref[c * 8 : (c + 1) * 8, heads * HEAD :] = stat.astype(bf16)


def merge_near_kernel(heads, s_ref, x_ref, o_ref, lse_ref, out_ref):
    merge(heads, x_ref, (s_ref[0], o_ref, lse_ref), out_ref, True)


def merge_far_kernel(heads, x_ref, out_ref):
    merge(heads, x_ref, None, out_ref, False)


def output_kernel(x_ref, w_ref, down_ref, up_ref, adapter_ref, out_ref):
    rows = adapter_ref.shape[1]
    half_width = x_ref.shape[1]
    i = lax.broadcasted_iota(jnp.int32, (rows, x_ref.shape[0]), 1)
    r = lax.broadcasted_iota(jnp.int32, (rows, x_ref.shape[0]), 0)
    near = NZM * NZP
    member = i // (2 * NZH)
    hit = r == (member // near) * (near * NZH) + lax.rem(i, NZH) * near + lax.rem(member, near)
    half = lax.rem(i // NZH, 2)
    across = (((1,), (1,)), ((), ()))
    plain = jnp.zeros((w_ref.shape[0], rows), f32)
    narrow = jnp.zeros((down_ref.shape[0], rows), f32)
    for k in range(2):
        pick = jnp.where(hit & (half == k), 1.0, 0.0).astype(bf16)
        x = jnp.dot(pick, x_ref[...], preferred_element_type=f32).astype(bf16)
        cols = slice(k * half_width, (k + 1) * half_width)
        plain = plain + lax.dot_general(w_ref[:, cols], x, across, preferred_element_type=f32)
        narrow = narrow + lax.dot_general(down_ref[:, cols], x, across, preferred_element_type=f32)
    column = lax.broadcasted_iota(jnp.int32, narrow.shape, 0)
    hi, lo = two_terms(jnp.where(column // LOW_RANK == adapter_ref[...], narrow, 0.0))
    up = up_ref[...]
    plain = plain + (
        jnp.dot(up, hi, preferred_element_type=f32) + jnp.dot(up, lo, preferred_element_type=f32)
    )
    count = w_ref.shape[0]
    for c in range(out_ref.shape[0] // count):
        out_ref[c * count : (c + 1) * count, :] = plain


def cached_part(query, old_keys, old_values, old_length, last_key, last_value):
    group = HEADS // KV_HEADS
    q = query.reshape(-1, group, HEAD)
    kv = q.shape[0]
    scale = HEAD ** (-0.5)

    def score_of(keys):
        shaped = keys.reshape(keys.shape[0], kv, HEAD)
        return jnp.einsum("kgd,lkd->kgl", q, shaped, preferred_element_type=f32) * scale

    def mix_with(weights, values):
        shaped = values.reshape(values.shape[0], kv, HEAD)
        return jnp.einsum("kgl,lkd->kgd", weights, shaped, preferred_element_type=f32)

    valid = jnp.arange(old_keys.shape[0], dtype=jnp.int32) < old_length
    old = jnp.where(valid[None, None, :], score_of(old_keys), NEG)
    last = score_of(last_key[None, :])
    top = jnp.maximum(jnp.max(old, axis=-1, keepdims=True), last)
    old_w = jnp.exp(old - top)
    last_w = jnp.exp(last - top)
    total = jnp.sum(old_w, axis=-1, keepdims=True) + last_w
    o = mix_with((old_w / total).astype(bf16), old_values)
    o = o + mix_with((last_w / total).astype(bf16), last_value[None, :])
    lse = (top + jnp.log(total)).reshape(kv, -1)
    return o.reshape(kv, -1), jnp.pad(lse, ((0, 0), (0, HEAD - lse.shape[1])))


def per_device(
    prompt_activations,
    key_matrix,
    value_matrix,
    adapter_down_keyvalue,
    adapter_up_key,
    adapter_up_value,
    request_adapter,
    page_request,
    context_tokens,
    step_query,
    step_key,
    step_value,
    stored_keys,
    stored_values,
    output_matrix,
    adapter_down_output,
    adapter_up_output,
):
    device = lax.axis_index(DEV)
    me = lax.axis_index("x").astype(jnp.int32)
    parity = lax.axis_index("zp").astype(jnp.int32)
    zh = lax.axis_index("zh").astype(jnp.int32)
    tokens = prompt_activations.shape[0]
    pages = tokens // PAGE
    requests = request_adapter.shape[0]
    kv = key_matrix.shape[1] // HEAD
    heads = step_query.shape[1] // HEAD
    depth = key_matrix.shape[0]
    width = 2 * key_matrix.shape[1] + adapter_down_keyvalue.shape[1]

    weights = jnp.concatenate([key_matrix, value_matrix, adapter_down_keyvalue], axis=1)
    query_rows = jnp.pad(step_query.reshape(4, -1), ((0, 4), (0, width - step_query.shape[1] // 4)))
    block = jnp.concatenate([weights, query_rows], axis=0)
    column = lax.all_gather(block, Z8)
    count = column.shape[0]
    chunks = 2
    per_chunk = count // chunks
    pieces = []
    for c in range(chunks):
        part = column[c * per_chunk : (c + 1) * per_chunk]
        pieces.append(
            jnp.concatenate(
                [
                    part[:, :depth].reshape(per_chunk * depth, width),
                    part[:, depth : depth + 4].reshape(per_chunk * 4, width),
                ],
                axis=0,
            )
        )
    chunk_depth = per_chunk * depth

    activations, _ = lax.optimization_barrier((prompt_activations, column))
    mine, theirs = split_columns(activations, parity[None])
    partner_act = swap_pair(theirs)

    by_offset = {0: pieces}
    ahead = behind = pieces
    for s in range(1, NX // 2):
        ahead = [ring_x(a, 1) for a in ahead]
        behind = [ring_x(b, -1) for b in behind]
        by_offset[NX - s] = ahead
        by_offset[s] = behind
    by_offset[NX // 2] = [ring_x(ahead[0], 1), ring_x(behind[1], -1)]
    offsets = (0, 7, 1, 6, 2, 5, 3, 4)
    flat = [a for off in range(NX) for a in by_offset[off]]
    ordered = [a for off in offsets for a in by_offset[off]]

    quarter = step_query.shape[1] // 4
    own_queries = collect_tails(flat, chunk_depth, quarter)
    pair_queries = swap_pair(own_queries)

    partial_other = project(partner_act, offsets, ordered, chunk_depth, me[None], bf16)
    from_partner = swap_pair(partial_other)
    base = project(mine, offsets, ordered, chunk_depth, me[None], f32)

    owners = page_request[:, 0]
    first_page = device * pages
    my_owners = lax.dynamic_slice_in_dim(owners, first_page, pages, 0)
    before = jnp.arange(owners.shape[0], dtype=jnp.int32)[None, :] < (
        first_page + jnp.arange(pages, dtype=jnp.int32)
    )[:, None]
    same = owners[None, :] == my_owners[:, None]
    rank = jnp.sum((same & before).astype(jnp.int32), axis=1)
    onehot = my_owners[:, None] == jnp.arange(requests, dtype=jnp.int32)[None, :]
    start = jnp.sum(jnp.where(onehot, context_tokens[None, :], 0), axis=1)
    adapter = jnp.sum(jnp.where(onehot, request_adapter[None, :], 0), axis=1)
    near = NZH * NZM * NZP
    z = my_owners % near
    z_low = z % (NZM * NZP)
    owner_spot = ((my_owners // near) * (NZM * NZP) + z_low) * (2 * NZH) + z // (NZM * NZP)
    inside = jnp.arange(PAGE, dtype=jnp.int32)[None, :]
    position = ((start + rank * PAGE)[:, None] + inside).reshape(-1)
    token_adapter = jnp.broadcast_to(adapter[:, None], (pages, PAGE)).reshape(-1, 1)
    token_owner = jnp.broadcast_to(owner_spot[:, None], (pages, PAGE)).reshape(1, -1)
    half = HEAD // 2
    exponent = jnp.arange(half, dtype=f32) * (2.0 / HEAD)
    frequency = jnp.exp(-jnp.log(jnp.float32(rope_base)) * exponent)
    angles = position.astype(f32)[:, None] * frequency[None, :]
    cosine, sine = jnp.cos(angles), jnp.sin(angles)
    cosine = jnp.concatenate([cosine, cosine], axis=1)
    sine = jnp.concatenate([-sine, sine], axis=1)

    cache_o, cache_lse = cached_part(
        step_query[0],
        stored_keys[0],
        stored_values[0],
        jnp.sum(jnp.where(jnp.arange(requests) == device, context_tokens, 0)),
        step_key[0],
        step_value[0],
    )

    half_heads = heads // kv
    half_width = half_heads * HEAD
    full_width = half_width + HEAD
    members = NX * NZM * NZP
    unit = kv * NZH
    payload = pl.pallas_call(
        functools.partial(partial_kernel, half_heads, kv),
        in_specs=[SMEM] + [VMEM] * 10,
        out_specs=VMEM,
        out_shape=jax.ShapeDtypeStruct((members * unit, full_width), bf16),
        name="partial_attention",
    )(
        jnp.stack([me, parity]), base, from_partner, adapter_up_key, adapter_up_value,
        cosine, sine, token_adapter, token_owner, own_queries, pair_queries,
    )
    arrived = lax.all_to_all(payload.reshape(members, unit, full_width), NEAR, 0, 0, tiled=True)
    merged = pl.pallas_call(
        functools.partial(merge_near_kernel, half_heads),
        in_specs=[SMEM] + [VMEM] * 3,
        out_specs=VMEM,
        out_shape=jax.ShapeDtypeStruct((NZH * unit, full_width), bf16),
        name="merge_near",
    )(zh[None], arrived.reshape(members * unit, full_width), cache_o, cache_lse)
    across = lax.all_to_all(merged.reshape(NZH, unit, full_width), "zh", 0, 0, tiled=True)
    mixed = pl.pallas_call(
        functools.partial(merge_far_kernel, half_heads),
        in_specs=[VMEM],
        out_specs=VMEM,
        out_shape=jax.ShapeDtypeStruct((members * unit, half_width), bf16),
        name="merge_far",
    )(across.reshape(NZH * unit, full_width))
    rows = lax.all_to_all(mixed.reshape(members, unit, half_width), NEAR, 0, 0, tiled=True)
    pair = lax.axis_size("tp")
    columns = output_matrix.shape[1]
    partial_output = pl.pallas_call(
        output_kernel,
        in_specs=[VMEM] * 5,
        out_specs=VMEM,
        out_shape=jax.ShapeDtypeStruct((pair * columns, requests), f32),
        name="output_rows",
    )(
        rows.reshape(members * unit, half_width), output_matrix.T, adapter_down_output.T,
        adapter_up_output.T, request_adapter[None, :],
    )
    everything = lax.all_to_all(
        partial_output.reshape(pair, columns, requests), "tp", 0, 0, tiled=True
    )
    return jnp.sum(everything, axis=0).T.astype(bf16)


def solution(mesh):
    finer = Mesh(
        mesh.devices.reshape(mesh.shape["group"], NX, NZH, NZM, NZP, mesh.shape["tp"]),
        ("group", "x", "zh", "zm", "zp", "tp"),
    )
    placed = (
        P(GROUP_DEV, None),
        P(DEV, "tp"),
        P(DEV, "tp"),
        P(DEV, None),
        P(None, "tp"),
        P(None, "tp"),
        P("group"),
        P("group", None),
        P("group"),
        P(GROUP_DEV, "tp"),
        P(GROUP_DEV, "tp"),
        P(GROUP_DEV, "tp"),
        P(GROUP_DEV, None, "tp"),
        P(GROUP_DEV, None, "tp"),
        P("tp", DEV),
        P("tp", None),
        P(None, DEV),
    )
    return jax.shard_map(
        per_device, mesh=finer, in_specs=placed, out_specs=P("group", DEV), check_vma=False
    )
```

profile of v0, /device:TPU:65, one launch (start us, length us, event | category | flops | bytes accessed | tf_op | source)
XLA Modules:
  0.0 252.7 jit_solution(6471542073892112668)
XLA Ops:
  0.0 0.7 reduce
  0.8 0.8 fusion.6
  1.6 64.2 %all-gather = bf16[576,640]{1,0:T(8,128)(2,1)S(1)} all-gather(bf16[72,640]{1,0:T(8,128)(2,1)S(1)} %fusion.6), channel_id=2, replica_groups=mesh['group'=2,'x'=8,'zh'=4,'zm'=2,'zp'=2,'tp'=2] {'zh','zm'}, dimensions={0}, use_global_device_ids=true | all-gather | bytes 829440 | tf_op jit(solution)/shard_map/all_gather | solution.py:366
  65.8 5.7 %split_columns.1 = (bf16[256,4096]{1,0:T(8,128)(2,1)}, bf16[256,4096]{1,0:T(8,128)(2,1)}) custom-call(s32[1]{0:T(128)} %bitcast.2.p_ref, bf16[256,8192]{1,0:T(8,128)(2,1)} %a_ref), custom_call_target="tpu_custom_call" | custom-call | tf_op jit(solution)/shard_map/split_columns/pallas_call | solution.py:63
  71.6 2.7 %collective-permute-start.14 = (bf16[256,4096]{1,0:T(8,128)(2,1)}, bf16[256,4096]{1,0:T(8,128)(2,1)}, u32[]{:S(2)}, u32[]{:S(2)}) collective-permute-start(bf16[256,4096]{1,0:T(8,128)(2,1)} %get-tuple-element.10), channel_id=1, source_target_pairs={{0,2},{2,0},{1,3},{3,1},{4,6},{6,4},{5,7},{7,5},{8,10},{10,8},{9,1... | collective-permute-start | bytes 6291464 | tf_op jit(solution)/shard_map/ppermute | solution.py:40
  74.4 4.9 %collective-permute-start = (bf16[272,640]{1,0:T(8,128)(2,1)S(1)}, bf16[272,640]{1,0:T(8,128)(2,1)S(1)}, u32[]{:S(2)}, u32[]{:S(2)}) collective-permute-start(bf16[272,640]{1,0:T(8,128)(2,1)S(1)} %pad_maximum_fusion.refs_0_), channel_id=1, source_target_pairs={{0,32},{32,64},{64,96},{96,128},{128,160},{160,192},{192,224},{224... | collective-permute-start | bytes 1044488 | tf_op jit(solution)/shard_map/ppermute | solution.py:36
  79.4 4.1 %collective-permute-start.3 = (bf16[272,640]{1,0:T(8,128)(2,1)S(1)}, bf16[272,640]{1,0:T(8,128)(2,1)S(1)}, u32[]{:S(2)}, u32[]{:S(2)}) collective-permute-start(bf16[272,640]{1,0:T(8,128)(2,1)S(1)} %pad_maximum_fusion.1.refs_1_), channel_id=1, source_target_pairs={{0,224},{32,0},{64,32},{96,64},{128,96},{160,128},{192,160},{224,1... | collective-permute-start | bytes 1044488 | tf_op jit(solution)/shard_map/ppermute | solution.py:36
  83.5 2.0 collective-permute-start.1
  85.5 4.6 %collective-permute-start.2 = (bf16[272,640]{1,0:T(8,128)(2,1)S(1)}, bf16[272,640]{1,0:T(8,128)(2,1)S(1)}, u32[]{:S(2)}, u32[]{:S(2)}) collective-permute-start(bf16[272,640]{1,0:T(8,128)(2,1)S(1)} %pad_maximum_fusion.refs_0_), channel_id=1, source_target_pairs={{0,224},{32,0},{64,32},{96,64},{128,96},{160,128},{192,160},{224,1... | collective-permute-start | bytes 1044488 | tf_op jit(solution)/shard_map/ppermute | solution.py:36
  90.1 2.0 collective-permute-start.4
  92.1 4.6 %collective-permute-start.7 = (bf16[272,640]{1,0:T(8,128)(2,1)S(1)}, bf16[272,640]{1,0:T(8,128)(2,1)S(1)}, u32[]{:S(2)}, u32[]{:S(2)}) collective-permute-start(bf16[272,640]{1,0:T(8,128)(2,1)S(1)} %collective-permute-done.3.refs_5_.refs_3_), channel_id=1, source_target_pairs={{0,224},{32,0},{64,32},{96,64},{128,96},{160,128},{192,160},{224,1... | collective-permute-start | bytes 1044488 | tf_op jit(solution)/shard_map/ppermute | solution.py:36
  96.8 2.0 collective-permute-start.5
  98.8 4.6 %collective-permute-start.6 = (bf16[272,640]{1,0:T(8,128)(2,1)S(1)}, bf16[272,640]{1,0:T(8,128)(2,1)S(1)}, u32[]{:S(2)}, u32[]{:S(2)}) collective-permute-start(bf16[272,640]{1,0:T(8,128)(2,1)S(1)} %collective-permute-done.2.refs_4_.refs_2_), channel_id=1, source_target_pairs={{0,224},{32,0},{64,32},{96,64},{128,96},{160,128},{192,160},{224,1... | collective-permute-start | bytes 1044488 | tf_op jit(solution)/shard_map/ppermute | solution.py:36
  103.7 1.9 collective-permute-start.8
  105.6 5.0 %collective-permute-start.11 = (bf16[272,640]{1,0:T(8,128)(2,1)S(1)}, bf16[272,640]{1,0:T(8,128)(2,1)}, u32[]{:S(2)}, u32[]{:S(2)}) collective-permute-start(bf16[272,640]{1,0:T(8,128)(2,1)S(1)} %collective-permute-done.7.refs_9_.refs_5_), channel_id=1, source_target_pairs={{0,224},{32,0},{64,32},{96,64},{128,96},{160,128},{192,160},{224,1... | collective-permute-start | bytes 1044488 | tf_op jit(solution)/shard_map/ppermute | solution.py:36
  110.8 0.6 convert_reduce_fusion
  111.5 2.0 collective-permute-start.9
  113.5 4.6 %collective-permute-start.10 = (bf16[272,640]{1,0:T(8,128)(2,1)S(1)}, bf16[272,640]{1,0:T(8,128)(2,1)}, u32[]{:S(2)}, u32[]{:S(2)}) collective-permute-start(bf16[272,640]{1,0:T(8,128)(2,1)S(1)} %collective-permute-done.6.refs_8_.refs_4_), channel_id=1, source_target_pairs={{0,224},{32,0},{64,32},{96,64},{128,96},{160,128},{192,160},{224,1... | collective-permute-start | bytes 1044488 | tf_op jit(solution)/shard_map/ppermute | solution.py:36
  118.7 1.9 collective-permute-start.12
  120.6 5.0 %collective-permute-start.13 = (bf16[272,640]{1,0:T(8,128)(2,1)}, bf16[272,640]{1,0:T(8,128)(2,1)}, u32[]{:S(2)}, u32[]{:S(2)}) collective-permute-start(bf16[272,640]{1,0:T(8,128)(2,1)} %collective-permute-done.11.refs_13_.refs_7_), channel_id=1, source_target_pairs={{0,224},{32,0},{64,32},{96,64},{128,96},{160,128},{192,160},{224,1... | collective-permute-start | bytes 1044488 | tf_op jit(solution)/shard_map/ppermute | solution.py:36
  126.1 1.5 collective-permute-done.10.refs_12_.refs_6_
  127.7 5.9 %collective-permute-done.12.refs_14_.refs_8_ = bf16[272,640]{1,0:T(8,128)(2,1)} collective-permute-done((bf16[272,640]{1,0:T(8,128)(2,1)}, bf16[272,640]{1,0:T(8,128)(2,1)}, u32[]{:S(2)}, u32[]{:S(2)}) %collective-permute-start.12) | collective-permute-done | bytes 348192 | tf_op jit(solution)/shard_map/ppermute | solution.py:36
  133.6 1.6 collective-permute-done.13.refs_15_.refs_9_
  135.3 1.6 collect_tails.1.q0_ref
  137.0 1.9 collective-permute-start.16
  138.9 8.6 %project.3 = bf16[256,640]{1,0:T(8,128)(2,1)} custom-call(s32[1]{0:T(128)} %bitcast.1.x_ref, bf16[256,4096]{1,0:T(8,128)(2,1)} %collective-permute-done.14.a_ref, bf16[272,640]{1,0:T(8,128)(2,1)} %copy-done.1, bf16[272,640]{1,0:T(8,128)(2,1)} %copy-done.2, bf16[272,640]{1,0:T(8,128)(2,1)} %copy-done.3, bf16[272,640]{1,0:T(8,128)(2,1)} %copy-done.5, ...), custom_call_target="tpu_custom_call" | custom-call | tf_op jit(solution)/shard_map/project/pallas_call | solution.py:101
  147.5 3.6 %collective-permute-start.15 = (bf16[256,640]{1,0:T(8,128)(2,1)}, bf16[256,640]{1,0:T(8,128)(2,1)S(1)}, u32[]{:S(2)}, u32[]{:S(2)}) collective-permute-start(bf16[256,640]{1,0:T(8,128)(2,1)} %project.3), channel_id=1, source_target_pairs={{0,2},{2,0},{1,3},{3,1},{4,6},{6,4},{5,7},{7,5},{8,10},{10,8},{9,1... | collective-permute-start | bytes 983048 | tf_op jit(solution)/shard_map/ppermute | solution.py:40
  151.7 0.8 reshape.132.adapter_ref
  152.5 0.7 reshape.117.owner_ref
  153.2 0.6 pad_add_fusion.s_ref
  153.8 0.8 pad_maximum_fusion.2
  154.6 8.7 %project.2.base_ref = f32[256,640]{1,0:T(8,128)} custom-call(s32[1]{0:T(128)} %bitcast.1.x_ref, bf16[256,4096]{1,0:T(8,128)(2,1)} %get-tuple-element.9.a_ref, bf16[272,640]{1,0:T(8,128)(2,1)} %copy-done.1, bf16[272,640]{1,0:T(8,128)(2,1)} %copy-done.2, bf16[272,640]{1,0:T(8,128)(2,1)} %copy-done.3, bf16[272,640]{1,0:T(8,128)(2,1)} %copy-done.5, ...), custom_call_target="tpu_custom_call" | custom-call | tf_op jit(solution)/shard_map/project/pallas_call | solution.py:101
  163.4 0.7 copy-done.14
  164.2 6.0 %partial_attention.1 = bf16[256,1152]{1,0:T(8,128)(2,1)} custom-call(s32[2]{0:T(128)} %pad_add_fusion.s_ref, f32[256,640]{1,0:T(8,128)} %project.2.base_ref, bf16[256,640]{1,0:T(8,128)(2,1)} %copy-done.13, bf16[64,256]{1,0:T(8,128)(2,1)} %upk_ref.1, bf16[64,256]{1,0:T(8,128)(2,1)} %upv_ref.1, f32[256,128]{1,0:T(8,128)} %get-tuple-element.26.cos_ref, ...), custom_call_target="tpu_custom_call" | custom-call | tf_op jit(solution)/shard_map/partial_attention/pallas_call | solution.py:449
  170.2 8.1 %all-to-all-start = ((bf16[32,8,1152]{2,1,0:T(8,128)(2,1)}), bf16[32,8,1152]{2,1,0:T(8,128)(2,1)S(1)}, u32[]{:S(2)}, u32[]{:S(2)}) async-start(bf16[32,8,1152]{2,1,0:T(8,128)(2,1)} %bitcast.46), calls=%async_computation | async-start | bytes 1179648 | tf_op jit(solution)/shard_map/all_to_all | solution.py:459
  178.4 0.6 fusion.16
  179.0 0.6 iota_compare_fusion.3
  181.6 9.4 %all-to-all-done = bf16[32,8,1152]{2,1,0:T(8,128)(2,1)S(1)} async-done(((bf16[32,8,1152]{2,1,0:T(8,128)(2,1)}), bf16[32,8,1152]{2,1,0:T(8,128)(2,1)S(1)}, u32[]{:S(2)}, u32[]{:S(2)}) %all-to-all-start) | async-done | bytes 589856 | tf_op jit(solution)/shard_map/all_to_all | solution.py:459
  191.0 0.8 copy-done.11
  191.8 2.2 merge_near.1
  194.0 20.0 %all_to_all.20 = bf16[4,8,1152]{2,1,0:T(8,128)(2,1)} all-to-all(bf16[4,8,1152]{2,1,0:T(8,128)(2,1)} %bitcast.51), channel_id=1, replica_groups=mesh['group'=2,'x'=8,'zh'=4,'zm'=2,'zp'=2,'tp'=2] {'zh'}, dimensions={0} | all-to-all | bytes 147456 | tf_op jit(solution)/shard_map/all_to_all | solution.py:467
  214.0 2.0 merge_far.1
  216.0 4.8 %all-to-all-start.2 = ((bf16[32,8,1024]{2,1,0:T(8,128)(2,1)}), bf16[32,8,1024]{2,1,0:T(8,128)(2,1)S(1)}, u32[]{:S(2)}, u32[]{:S(2)}) async-start(bf16[32,8,1024]{2,1,0:T(8,128)(2,1)} %bitcast.48), calls=%async_computation.2 | async-start | bytes 1048576 | tf_op jit(solution)/shard_map/all_to_all | solution.py:475
  220.9 0.7 copy.28
  221.6 11.4 %all-to-all-done.2 = bf16[32,8,1024]{2,1,0:T(8,128)(2,1)S(1)} async-done(((bf16[32,8,1024]{2,1,0:T(8,128)(2,1)}), bf16[32,8,1024]{2,1,0:T(8,128)(2,1)S(1)}, u32[]{:S(2)}, u32[]{:S(2)}) %all-to-all-start.2) | async-done | bytes 524320 | tf_op jit(solution)/shard_map/all_to_all | solution.py:475
  232.9 0.8 copy-done.12
  233.7 2.7 %output_rows.1 = f32[128,128]{1,0:T(8,128)} custom-call(bf16[256,1024]{1,0:T(8,128)(2,1)} %bitcast.47, bf16[64,2048]{1,0:T(8,128)(2,1)} %bitcast.54, bf16[64,2048]{1,0:T(8,128)(2,1)} %bitcast.55, bf16[64,64]{1,0:T(8,128)(2,1)} %bitcast.56, s32[1,128]{1,0:T(1,128)} %bitcast.62), custom_call_target="tpu_custom_call" | custom-call | tf_op jit(solution)/shard_map/output_rows/pallas_call | solution.py:478
  236.4 15.7 %all_to_all.21 = f32[2,64,128]{2,1,0:T(8,128)S(1)} all-to-all(f32[2,64,128]{2,1,0:T(8,128)} %bitcast.53), channel_id=1, replica_groups=mesh['group'=2,'x'=8,'zh'=4,'zm'=2,'zp'=2,'tp'=2] {'tp'}, dimensions={0} | all-to-all | bytes 131072 | tf_op jit(solution)/shard_map/all_to_all | solution.py:488
  (85 shorter events, 5.2 us)
Async XLA Ops:
  0.0 179.7 %copy-start = (bf16[1,256]{1,0:T(2,128)(2,1)S(1)}, bf16[1,256]{1,0:T(2,128)(2,1)}, u32[]{:S(2)}) copy-start(bf16[1,256]{1,0:T(2,128)(2,1)} %param.27) | copy-start | bytes 1540
  71.5 25.2 %copy-start.17 = (s32[8192,1]{0,1:T(1,128)S(1)}, s32[8192,1]{0,1:T(1,128)}, u32[]{:S(2)}) copy-start(s32[8192,1]{0,1:T(1,128)} %param.24) | copy-start | bytes 98308
  71.6 39.1 %copy-start.19 = (s32[128]{0:T(128)S(1)}, s32[128]{0:T(128)}, u32[]{:S(2)}) copy-start(s32[128]{0:T(128)} %param.23) | copy-start | bytes 1540
  71.6 39.1 %copy-start.21 = (s32[128]{0:T(128)S(1)}, s32[128]{0:T(128)}, u32[]{:S(2)}) copy-start(s32[128]{0:T(128)} %param.25) | copy-start | bytes 1540
  71.6 67.3 %collective-permute-start.14 = (bf16[256,4096]{1,0:T(8,128)(2,1)}, bf16[256,4096]{1,0:T(8,128)(2,1)}, u32[]{:S(2)}, u32[]{:S(2)}) collective-permute-start(bf16[256,4096]{1,0:T(8,128)(2,1)} %get-tuple-element.10), channel_id=1, source_target_pairs={{0,2},{2,0},{1,3},{3,1},{4,6},{6,4},{5,7},{7,5},{8,10},{10,8},{9,1... | collective-permute-start | bytes 6291464 | tf_op jit(solution)/shard_map/ppermute | solution.py:40
  74.4 60.9 %copy-start.1 = (bf16[272,640]{1,0:T(8,128)(2,1)}, bf16[272,640]{1,0:T(8,128)(2,1)S(1)}, u32[]{:S(2)}) copy-start(bf16[272,640]{1,0:T(8,128)(2,1)S(1)} %pad_maximum_fusion.refs_0_) | copy-start | bytes 1044484
  74.4 15.7 %collective-permute-start = (bf16[272,640]{1,0:T(8,128)(2,1)S(1)}, bf16[272,640]{1,0:T(8,128)(2,1)S(1)}, u32[]{:S(2)}, u32[]{:S(2)}) collective-permute-start(bf16[272,640]{1,0:T(8,128)(2,1)S(1)} %pad_maximum_fusion.refs_0_), channel_id=1, source_target_pairs={{0,32},{32,64},{64,96},{96,128},{128,160},{160,192},{192,224},{224... | collective-permute-start | bytes 1044488 | tf_op jit(solution)/shard_map/ppermute | solution.py:36
  79.3 55.9 %copy-start.2 = (bf16[272,640]{1,0:T(8,128)(2,1)}, bf16[272,640]{1,0:T(8,128)(2,1)S(1)}, u32[]{:S(2)}) copy-start(bf16[272,640]{1,0:T(8,128)(2,1)S(1)} %pad_maximum_fusion.1.refs_1_) | copy-start | bytes 1044484
  79.4 12.7 %collective-permute-start.3 = (bf16[272,640]{1,0:T(8,128)(2,1)S(1)}, bf16[272,640]{1,0:T(8,128)(2,1)S(1)}, u32[]{:S(2)}, u32[]{:S(2)}) collective-permute-start(bf16[272,640]{1,0:T(8,128)(2,1)S(1)} %pad_maximum_fusion.1.refs_1_), channel_id=1, source_target_pairs={{0,224},{32,0},{64,32},{96,64},{128,96},{160,128},{192,160},{224,1... | collective-permute-start | bytes 1044488 | tf_op jit(solution)/shard_map/ppermute | solution.py:36
  83.5 13.3 %collective-permute-start.1 = (bf16[272,640]{1,0:T(8,128)(2,1)S(1)}, bf16[272,640]{1,0:T(8,128)(2,1)S(1)}, u32[]{:S(2)}, u32[]{:S(2)}) collective-permute-start(bf16[272,640]{1,0:T(8,128)(2,1)S(1)} %pad_maximum_fusion.1.refs_1_), channel_id=1, source_target_pairs={{0,32},{32,64},{64,96},{96,128},{128,160},{160,192},{192,224},{224... | collective-permute-start | bytes 1044488 | tf_op jit(solution)/shard_map/ppermute | solution.py:36
  85.5 13.3 %collective-permute-start.2 = (bf16[272,640]{1,0:T(8,128)(2,1)S(1)}, bf16[272,640]{1,0:T(8,128)(2,1)S(1)}, u32[]{:S(2)}, u32[]{:S(2)}) collective-permute-start(bf16[272,640]{1,0:T(8,128)(2,1)S(1)} %pad_maximum_fusion.refs_0_), channel_id=1, source_target_pairs={{0,224},{32,0},{64,32},{96,64},{128,96},{160,128},{192,160},{224,1... | collective-permute-start | bytes 1044488 | tf_op jit(solution)/shard_map/ppermute | solution.py:36
  90.1 45.2 %copy-start.3 = (bf16[272,640]{1,0:T(8,128)(2,1)}, bf16[272,640]{1,0:T(8,128)(2,1)S(1)}, u32[]{:S(2)}) copy-start(bf16[272,640]{1,0:T(8,128)(2,1)S(1)} %collective-permute-done.refs_2_.refs_14_) | copy-start | bytes 1044484
  90.1 13.6 %collective-permute-start.4 = (bf16[272,640]{1,0:T(8,128)(2,1)S(1)}, bf16[272,640]{1,0:T(8,128)(2,1)S(1)}, u32[]{:S(2)}, u32[]{:S(2)}) collective-permute-start(bf16[272,640]{1,0:T(8,128)(2,1)S(1)} %collective-permute-done.refs_2_.refs_14_), channel_id=1, source_target_pairs={{0,32},{32,64},{64,96},{96,128},{128,160},{160,192},{192,224},{224... | collective-permute-start | bytes 1044488 | tf_op jit(solution)/shard_map/ppermute | solution.py:36
  92.1 43.2 %copy-start.4 = (bf16[272,640]{1,0:T(8,128)(2,1)}, bf16[272,640]{1,0:T(8,128)(2,1)S(1)}, u32[]{:S(2)}) copy-start(bf16[272,640]{1,0:T(8,128)(2,1)S(1)} %collective-permute-done.3.refs_5_.refs_3_) | copy-start | bytes 1044484
  92.1 13.5 %collective-permute-start.7 = (bf16[272,640]{1,0:T(8,128)(2,1)S(1)}, bf16[272,640]{1,0:T(8,128)(2,1)S(1)}, u32[]{:S(2)}, u32[]{:S(2)}) collective-permute-start(bf16[272,640]{1,0:T(8,128)(2,1)S(1)} %collective-permute-done.3.refs_5_.refs_3_), channel_id=1, source_target_pairs={{0,224},{32,0},{64,32},{96,64},{128,96},{160,128},{192,160},{224,1... | collective-permute-start | bytes 1044488 | tf_op jit(solution)/shard_map/ppermute | solution.py:36
  96.8 38.4 %copy-start.5 = (bf16[272,640]{1,0:T(8,128)(2,1)}, bf16[272,640]{1,0:T(8,128)(2,1)S(1)}, u32[]{:S(2)}) copy-start(bf16[272,640]{1,0:T(8,128)(2,1)S(1)} %collective-permute-done.1.refs_3_.refs_15_) | copy-start | bytes 1044484
  96.8 14.7 %collective-permute-start.5 = (bf16[272,640]{1,0:T(8,128)(2,1)S(1)}, bf16[272,640]{1,0:T(8,128)(2,1)S(1)}, u32[]{:S(2)}, u32[]{:S(2)}) collective-permute-start(bf16[272,640]{1,0:T(8,128)(2,1)S(1)} %collective-permute-done.1.refs_3_.refs_15_), channel_id=1, source_target_pairs={{0,32},{32,64},{64,96},{96,128},{128,160},{160,192},{192,224},{224... | collective-permute-start | bytes 1044488 | tf_op jit(solution)/shard_map/ppermute | solution.py:36
  98.8 36.5 %copy-start.6 = (bf16[272,640]{1,0:T(8,128)(2,1)}, bf16[272,640]{1,0:T(8,128)(2,1)S(1)}, u32[]{:S(2)}) copy-start(bf16[272,640]{1,0:T(8,128)(2,1)S(1)} %collective-permute-done.2.refs_4_.refs_2_) | copy-start | bytes 1044484
  98.8 14.7 %collective-permute-start.6 = (bf16[272,640]{1,0:T(8,128)(2,1)S(1)}, bf16[272,640]{1,0:T(8,128)(2,1)S(1)}, u32[]{:S(2)}, u32[]{:S(2)}) collective-permute-start(bf16[272,640]{1,0:T(8,128)(2,1)S(1)} %collective-permute-done.2.refs_4_.refs_2_), channel_id=1, source_target_pairs={{0,224},{32,0},{64,32},{96,64},{128,96},{160,128},{192,160},{224,1... | collective-permute-start | bytes 1044488 | tf_op jit(solution)/shard_map/ppermute | solution.py:36
  103.6 31.6 %copy-start.7 = (bf16[272,640]{1,0:T(8,128)(2,1)}, bf16[272,640]{1,0:T(8,128)(2,1)S(1)}, u32[]{:S(2)}) copy-start(bf16[272,640]{1,0:T(8,128)(2,1)S(1)} %collective-permute-done.4.refs_6_.refs_12_) | copy-start | bytes 1044484
  103.7 15.0 %collective-permute-start.8 = (bf16[272,640]{1,0:T(8,128)(2,1)S(1)}, bf16[272,640]{1,0:T(8,128)(2,1)}, u32[]{:S(2)}, u32[]{:S(2)}) collective-permute-start(bf16[272,640]{1,0:T(8,128)(2,1)S(1)} %collective-permute-done.4.refs_6_.refs_12_), channel_id=1, source_target_pairs={{0,32},{32,64},{64,96},{96,128},{128,160},{160,192},{192,224},{224... | collective-permute-start | bytes 1044488 | tf_op jit(solution)/shard_map/ppermute | solution.py:36
  105.6 29.7 %copy-start.8 = (bf16[272,640]{1,0:T(8,128)(2,1)}, bf16[272,640]{1,0:T(8,128)(2,1)S(1)}, u32[]{:S(2)}) copy-start(bf16[272,640]{1,0:T(8,128)(2,1)S(1)} %collective-permute-done.7.refs_9_.refs_5_) | copy-start | bytes 1044484
  105.6 15.0 %collective-permute-start.11 = (bf16[272,640]{1,0:T(8,128)(2,1)S(1)}, bf16[272,640]{1,0:T(8,128)(2,1)}, u32[]{:S(2)}, u32[]{:S(2)}) collective-permute-start(bf16[272,640]{1,0:T(8,128)(2,1)S(1)} %collective-permute-done.7.refs_9_.refs_5_), channel_id=1, source_target_pairs={{0,224},{32,0},{64,32},{96,64},{128,96},{160,128},{192,160},{224,1... | collective-permute-start | bytes 1044488 | tf_op jit(solution)/shard_map/ppermute | solution.py:36
  111.5 23.8 %copy-start.9 = (bf16[272,640]{1,0:T(8,128)(2,1)}, bf16[272,640]{1,0:T(8,128)(2,1)S(1)}, u32[]{:S(2)}) copy-start(bf16[272,640]{1,0:T(8,128)(2,1)S(1)} %collective-permute-done.5.refs_7_.refs_13_) | copy-start | bytes 1044484
  111.5 14.6 %collective-permute-start.9 = (bf16[272,640]{1,0:T(8,128)(2,1)S(1)}, bf16[272,640]{1,0:T(8,128)(2,1)}, u32[]{:S(2)}, u32[]{:S(2)}) collective-permute-start(bf16[272,640]{1,0:T(8,128)(2,1)S(1)} %collective-permute-done.5.refs_7_.refs_13_), channel_id=1, source_target_pairs={{0,32},{32,64},{64,96},{96,128},{128,160},{160,192},{192,224},{224... | collective-permute-start | bytes 1044488 | tf_op jit(solution)/shard_map/ppermute | solution.py:36
  113.5 21.8 %copy-start.10 = (bf16[272,640]{1,0:T(8,128)(2,1)}, bf16[272,640]{1,0:T(8,128)(2,1)S(1)}, u32[]{:S(2)}) copy-start(bf16[272,640]{1,0:T(8,128)(2,1)S(1)} %collective-permute-done.6.refs_8_.refs_4_) | copy-start | bytes 1044484
  113.5 14.2 %collective-permute-start.10 = (bf16[272,640]{1,0:T(8,128)(2,1)S(1)}, bf16[272,640]{1,0:T(8,128)(2,1)}, u32[]{:S(2)}, u32[]{:S(2)}) collective-permute-start(bf16[272,640]{1,0:T(8,128)(2,1)S(1)} %collective-permute-done.6.refs_8_.refs_4_), channel_id=1, source_target_pairs={{0,224},{32,0},{64,32},{96,64},{128,96},{160,128},{192,160},{224,1... | collective-permute-start | bytes 1044488 | tf_op jit(solution)/shard_map/ppermute | solution.py:36
  118.7 14.9 %collective-permute-start.12 = (bf16[272,640]{1,0:T(8,128)(2,1)}, bf16[272,640]{1,0:T(8,128)(2,1)}, u32[]{:S(2)}, u32[]{:S(2)}) collective-permute-start(bf16[272,640]{1,0:T(8,128)(2,1)} %collective-permute-done.8.refs_10_), channel_id=1, source_target_pairs={{0,32},{32,64},{64,96},{96,128},{128,160},{160,192},{192,224},{224... | collective-permute-start | bytes 1044488 | tf_op jit(solution)/shard_map/ppermute | solution.py:36
  120.6 14.6 %collective-permute-start.13 = (bf16[272,640]{1,0:T(8,128)(2,1)}, bf16[272,640]{1,0:T(8,128)(2,1)}, u32[]{:S(2)}, u32[]{:S(2)}) collective-permute-start(bf16[272,640]{1,0:T(8,128)(2,1)} %collective-permute-done.11.refs_13_.refs_7_), channel_id=1, source_target_pairs={{0,224},{32,0},{64,32},{96,64},{128,96},{160,128},{192,160},{224,1... | collective-permute-start | bytes 1044488 | tf_op jit(solution)/shard_map/ppermute | solution.py:36
  137.0 26.4 %collective-permute-start.16 = (bf16[256,512]{1,0:T(8,128)(2,1)}, bf16[256,512]{1,0:T(8,128)(2,1)S(1)}, u32[]{:S(2)}, u32[]{:S(2)}) collective-permute-start(bf16[256,512]{1,0:T(8,128)(2,1)} %collect_tails.1.q0_ref), channel_id=1, source_target_pairs={{0,2},{2,0},{1,3},{3,1},{4,6},{6,4},{5,7},{7,5},{8,10},{10,8},{9,1... | collective-permute-start | bytes 786440 | tf_op jit(solution)/shard_map/ppermute | solution.py:40
  147.5 15.9 %collective-permute-start.15 = (bf16[256,640]{1,0:T(8,128)(2,1)}, bf16[256,640]{1,0:T(8,128)(2,1)S(1)}, u32[]{:S(2)}, u32[]{:S(2)}) collective-permute-start(bf16[256,640]{1,0:T(8,128)(2,1)} %project.3), channel_id=1, source_target_pairs={{0,2},{2,0},{1,3},{3,1},{4,6},{6,4},{5,7},{7,5},{8,10},{10,8},{9,1... | collective-permute-start | bytes 983048 | tf_op jit(solution)/shard_map/ppermute | solution.py:40
  163.3 14.9 %copy-start.15 = (bf16[1,256,256]{2,1,0:T(8,128)(2,1)S(1)}, bf16[1,256,256]{2,1,0:T(8,128)(2,1)}, u32[]{:S(2)}) copy-start(bf16[1,256,256]{2,1,0:T(8,128)(2,1)} %param.30) | copy-start | bytes 393220
  163.3 15.0 %copy-start.16 = (bf16[1,256,256]{2,1,0:T(8,128)(2,1)S(1)}, bf16[1,256,256]{2,1,0:T(8,128)(2,1)}, u32[]{:S(2)}) copy-start(bf16[1,256,256]{2,1,0:T(8,128)(2,1)} %param.29) | copy-start | bytes 393220
  163.4 0.7 copy-start.14
  163.4 0.8 copy-start.13
  164.2 14.2 %copy-start.20 = (bf16[1,256]{1,0:T(2,128)(2,1)S(1)}, bf16[1,256]{1,0:T(2,128)(2,1)}, u32[]{:S(2)}) copy-start(bf16[1,256]{1,0:T(2,128)(2,1)} %param.28) | copy-start | bytes 1540
  170.2 50.7 %copy-start.18 = (bf16[64,64]{1,0:T(8,128)(2,1)S(1)}, bf16[64,64]{1,0:T(8,128)(2,1)}, u32[]{:S(2)}) copy-start(bf16[64,64]{1,0:T(8,128)(2,1)} %param.33) | copy-start | bytes 24580
  170.2 20.8 %all-to-all-start = ((bf16[32,8,1152]{2,1,0:T(8,128)(2,1)}), bf16[32,8,1152]{2,1,0:T(8,128)(2,1)S(1)}, u32[]{:S(2)}, u32[]{:S(2)}) async-start(bf16[32,8,1152]{2,1,0:T(8,128)(2,1)} %bitcast.46), calls=%async_computation | async-start | bytes 1179648 | tf_op jit(solution)/shard_map/all_to_all | solution.py:459
  191.0 0.8 copy-start.11
  216.0 16.9 %all-to-all-start.2 = ((bf16[32,8,1024]{2,1,0:T(8,128)(2,1)}), bf16[32,8,1024]{2,1,0:T(8,128)(2,1)S(1)}, u32[]{:S(2)}, u32[]{:S(2)}) async-start(bf16[32,8,1024]{2,1,0:T(8,128)(2,1)} %bitcast.48), calls=%async_computation.2 | async-start | bytes 1048576 | tf_op jit(solution)/shard_map/all_to_all | solution.py:475
  232.9 0.8 copy-start.12
where the time goes:
time: 254 us; the launch traced here: 253 us
  blocking collectives  99.9 us (39%)
  starting transfers between devices  70.2 us (28%)
  Pallas kernels  37.5 us (15%)
  waiting for transfers between devices  30.9 us (12%)
  other arithmetic  6.68 us (3%)
  local copies, waits for them, and re-layouts  6.28 us (2%)
    all_gather x1, blocking collectives, per_device(): column = lax.all_gather(block, Z8)  64.2 us
    ppermute x14, starting transfers between devices, ring_x(): return lax.ppermute(x, 'x', [(i, (i + step) % NX) for i in range(NX)])  49.1 us
    all_to_all x1, blocking collectives, per_device(): lax.all_to_all(merged.reshape(NZH, unit, full_width), 'zh', 0, 0, tiled=T...  20 us
    pallas_call x2, Pallas kernels, project(): pl.pallas_call(functools.partial(project_kernel, offsets, chunks, depth),...  17.2 us
    all_to_all x1, blocking collectives, per_device(): lax.all_to_all(partial_output.reshape(pair, columns, requests), 'tp', 0,...  15.7 us
    all_to_all x1, waiting for transfers between devices, per_device(): lax.all_to_all(mixed.reshape(members, unit, half_width), NEAR, 0, 0, tile...  11.4 us
    ppermute x14, waiting for transfers between devices, ring_x(): return lax.ppermute(x, 'x', [(i, (i + step) % NX) for i in range(NX)])  10.2 us
    all_to_all x1, waiting for transfers between devices, per_device(): lax.all_to_all(payload.reshape(members, unit, full_width), NEAR, 0, 0, ti...  9.37 us
  transfers between devices with their start and end apart: 19, of which 8 were waited for; matrix products, arithmetic and copies ran while one was open for 3% of the time, Pallas kernels for 7%

commit v1 on v0

--- a/solution.py
+++ b/solution.py
@@ -32,6 +32,10 @@
 VMEM = pl.BlockSpec(memory_space=pltpu.VMEM)
 
 
+def room(mib):
+    return pltpu.CompilerParams(vmem_limit_bytes=mib * 1024 * 1024)
+
+
 def ring_x(x, step):
     return lax.ppermute(x, "x", [(i, (i + step) % NX) for i in range(NX)])
 
@@ -41,24 +45,28 @@
 
 
 def split_kernel(p_ref, a_ref, mine_ref, other_ref):
-    parity = p_ref[0]
     half = HEAD // 2
-    lane = lax.broadcasted_iota(jnp.int32, (a_ref.shape[0], HEAD), 1)
-    low = lane < half
-    first = parity == 0
-    for k in range(mine_ref.shape[1] // HEAD):
-        t0 = a_ref[:, 2 * k * HEAD : (2 * k + 1) * HEAD].astype(f32)
-        t1 = a_ref[:, (2 * k + 1) * HEAD : (2 * k + 2) * HEAD].astype(f32)
-        even = jnp.where(low, t0, pltpu.roll(t1, half, 1))
-        odd = jnp.where(low, pltpu.roll(t0, half, 1), t1)
-        cols = slice(k * HEAD, (k + 1) * HEAD)
-        mine_ref[:, cols] = jnp.where(first, even, odd).astype(bf16)
-        other_ref[:, cols] = jnp.where(first, odd, even).astype(bf16)
+
+    def write(even_ref, odd_ref):
+        for k in range(even_ref.shape[1] // HEAD):
+            t0 = a_ref[:, 2 * k * HEAD : (2 * k + 1) * HEAD]
+            t1 = a_ref[:, (2 * k + 1) * HEAD : (2 * k + 2) * HEAD]
+            cols = slice(k * HEAD, (k + 1) * HEAD)
+            even_ref[:, cols] = jnp.concatenate([t0[:, :half], t1[:, :half]], axis=1)
+            odd_ref[:, cols] = jnp.concatenate([t0[:, half:], t1[:, half:]], axis=1)
+
+    @pl.when(p_ref[0] == 0)
+    def _():
+        write(mine_ref, other_ref)
+
+    @pl.when(p_ref[0] != 0)
+    def _():
+        write(other_ref, mine_ref)
 
 
 def split_columns(act, parity):
     rows, width = act.shape
-    block = 64
+    block = 32
     out = jax.ShapeDtypeStruct((rows, width // 2), bf16)
     return pl.pallas_call(
         split_kernel,
@@ -66,72 +74,60 @@
         in_specs=[SMEM, pl.BlockSpec((block, width), lambda i: (i, 0))],
         out_specs=[pl.BlockSpec((block, width // 2), lambda i: (i, 0))] * 2,
         out_shape=[out, out],
+        compiler_params=room(8),
         name="split_columns",
     )(parity, act)
 
 
 def project_kernel(offsets, chunks, depth, x_ref, a_ref, *refs):
-    count = len(offsets) * chunks
-    pieces, out_ref = refs[:count], refs[count]
-    a_buf, w_buf, a_sem, w_sem = refs[count + 1 :]
-    load_a = pltpu.make_async_copy(a_ref, a_buf, a_sem)
-    load_a.start()
-    loads = []
-    for j in range(count):
-        load = pltpu.make_async_copy(pieces[j].at[pl.ds(0, depth)], w_buf.at[j], w_sem.at[j])
-        load.start()
-        loads.append(load)
+    pieces, out_ref = refs[:-1], refs[-1]
     me = x_ref[0]
-    load_a.wait()
-    total = jnp.zeros(out_ref.shape, f32)
+    total = None
     for i, off in enumerate(offsets):
         where = lax.rem(me + off, NX)
-        for c in range(chunks):
-            start = pl.multiple_of((where * chunks + c) * depth, depth)
-            loads[i * chunks + c].wait()
-            a = a_buf[:, pl.ds(start, depth)]
-            total = total + jnp.dot(a, w_buf[i * chunks + c], preferred_element_type=f32)
+        start = pl.multiple_of(where * chunks * depth, chunks * depth)
+        a = a_ref[:, pl.ds(start, chunks * depth)]
+        w = jnp.concatenate(
+            [pieces[i * chunks + c][0:depth, :] for c in range(chunks)], axis=0
+        )
+        part = jnp.dot(a, w, preferred_element_type=f32)
+        total = part if total is None else total + part
     out_ref[...] = total.astype(out_ref.dtype)
 
 
 def project(act, offsets, pieces, depth, me, dtype):
     chunks = len(pieces) // len(offsets)
     width = pieces[0].shape[1]
-    anywhere = pl.BlockSpec(memory_space=pl.ANY)
     return pl.pallas_call(
         functools.partial(project_kernel, offsets, chunks, depth),
-        in_specs=[SMEM] + [anywhere] * (1 + len(pieces)),
+        in_specs=[SMEM] + [VMEM] * (1 + len(pieces)),
         out_specs=VMEM,
         out_shape=jax.ShapeDtypeStruct((act.shape[0], width), dtype),
-        scratch_shapes=[
-            pltpu.VMEM(act.shape, bf16),
-            pltpu.VMEM((len(pieces), depth, width), bf16),
-            pltpu.SemaphoreType.DMA,
-            pltpu.SemaphoreType.DMA((len(pieces),)),
-        ],
+        compiler_params=room(20),
         name="project",
     )(me, act, *pieces)
 
 
-def collect_kernel(*refs):
+def collect_kernel(after_ref, *refs):
     out_ref = refs[-1]
     rows, width = refs[0].shape[0], out_ref.shape[1]
     for j, ref in enumerate(refs[:-1]):
         out_ref[j * rows : (j + 1) * rows, :] = ref[:, :width]
 
 
-def collect_tails(pieces, depth, width):
+def collect_tails(pieces, depth, width, after):
     rows = pieces[0].shape[0] - depth
     tail = pl.BlockSpec((rows, pieces[0].shape[1]), lambda i: (depth // rows, 0))
     total = rows * len(pieces)
     return pl.pallas_call(
         collect_kernel,
         grid=(1,),
-        in_specs=[tail] * len(pieces),
+        in_specs=[pl.BlockSpec(memory_space=pl.ANY)] + [tail] * len(pieces),
         out_specs=pl.BlockSpec((total, width), lambda i: (0, 0)),
         out_shape=jax.ShapeDtypeStruct((total, width), bf16),
+        compiler_params=room(8),
         name="collect_tails",
-    )(*pieces)
+    )(after, *pieces)
 
 
 def two_terms(v):
@@ -398,11 +394,10 @@
     ordered = [a for off in offsets for a in by_offset[off]]
 
     quarter = step_query.shape[1] // 4
-    own_queries = collect_tails(flat, chunk_depth, quarter)
-    pair_queries = swap_pair(own_queries)
-
     partial_other = project(partner_act, offsets, ordered, chunk_depth, me[None], bf16)
     from_partner = swap_pair(partial_other)
+    own_queries = collect_tails(flat, chunk_depth, quarter, partial_other)
+    pair_queries = swap_pair(own_queries)
     base = project(mine, offsets, ordered, chunk_depth, me[None], f32)
 
     owners = page_request[:, 0]
@@ -451,6 +446,7 @@
         in_specs=[SMEM] + [VMEM] * 10,
         out_specs=VMEM,
         out_shape=jax.ShapeDtypeStruct((members * unit, full_width), bf16),
+        compiler_params=room(16),
         name="partial_attention",
     )(
         jnp.stack([me, parity]), base, from_partner, adapter_up_key, adapter_up_value,
@@ -462,6 +458,7 @@
         in_specs=[SMEM] + [VMEM] * 3,
         out_specs=VMEM,
         out_shape=jax.ShapeDtypeStruct((NZH * unit, full_width), bf16),
+        compiler_params=room(12),
         name="merge_near",
     )(zh[None], arrived.reshape(members * unit, full_width), cache_o, cache_lse)
     across = lax.all_to_all(merged.reshape(NZH, unit, full_width), "zh", 0, 0, tiled=True)
@@ -470,6 +467,7 @@
         in_specs=[VMEM],
         out_specs=VMEM,
         out_shape=jax.ShapeDtypeStruct((members * unit, half_width), bf16),
+        compiler_params=room(12),
         name="merge_far",
     )(across.reshape(NZH * unit, full_width))
     rows = lax.all_to_all(mixed.reshape(members, unit, half_width), NEAR, 0, 0, tiled=True)
@@ -480,6 +478,7 @@
         in_specs=[VMEM] * 5,
         out_specs=VMEM,
         out_shape=jax.ShapeDtypeStruct((pair * columns, requests), f32),
+        compiler_params=room(12),
         name="output_rows",
     )(
         rows.reshape(members * unit, half_width), output_matrix.T, adapter_down_output.T,

time: 254 us -> 239 us (0.941)
  Pallas kernels: 37.5 us -> 21.7 us
  blocking collectives: 99.9 us -> 95.2 us
  starting transfers between devices: 70.2 us -> 72.8 us
    pallas_call x2, Pallas kernels: 17.2 us -> 8.06 us  [project(): pl.pallas_call(functools.partial(project_kernel, offsets, chunks, depth),...]
    all_to_all x1, blocking collectives: 15.7 us -> 11.2 us  [per_device(): lax.all_to_all(partial_output.reshape(pair, columns, requests), 'tp', 0,...]
    all_to_all x1, starting transfers between devices: 4.8 us -> 7.63 us  [per_device(): lax.all_to_all(mixed.reshape(members, unit, half_width), NEAR, 0, 0, tile...]
    unnamed x46 -> x34, local copies, waits for them, and re-layouts: 3.83 us -> 5.25 us
  transfers between devices with their start and end apart: 19 -> 19, of which waited for: 8 -> 8; matrix products, arithmetic and copies ran while one was open for 3% -> 3% of each run, Pallas kernels for 7% -> 2%
where the time goes in v1:
time: 239 us; the launch traced here: 238 us
  blocking collectives  95.2 us (40%)
  starting transfers between devices  72.8 us (30%)
  waiting for transfers between devices  33.1 us (14%)
  Pallas kernels  21.7 us (9%)
  other arithmetic  7.34 us (3%)
  local copies, waits for them, and re-layouts  6.55 us (3%)
    all_gather x1, blocking collectives, per_device(): column = lax.all_gather(block, Z8)  64.2 us
    ppermute x14, starting transfers between devices, ring_x(): return lax.ppermute(x, 'x', [(i, (i + step) % NX) for i in range(NX)])  49.1 us
    all_to_all x1, blocking collectives, per_device(): lax.all_to_all(merged.reshape(NZH, unit, full_width), 'zh', 0, 0, tiled=T...  19.8 us
    all_to_all x1, waiting for transfers between devices, per_device(): lax.all_to_all(mixed.reshape(members, unit, half_width), NEAR, 0, 0, tile...  12.2 us
    all_to_all x1, blocking collectives, per_device(): lax.all_to_all(partial_output.reshape(pair, columns, requests), 'tp', 0,...  11.2 us
    all_to_all x1, waiting for transfers between devices, per_device(): lax.all_to_all(payload.reshape(members, unit, full_width), NEAR, 0, 0, ti...  10.5 us
    ppermute x14, waiting for transfers between devices, ring_x(): return lax.ppermute(x, 'x', [(i, (i + step) % NX) for i in range(NX)])  10.3 us
    all_to_all x1, starting transfers between devices, per_device(): lax.all_to_all(payload.reshape(members, unit, full_width), NEAR, 0, 0, ti...  8.07 us
  transfers between devices with their start and end apart: 19, of which 8 were waited for; matrix products, arithmetic and copies ran while one was open for 3% of the time, Pallas kernels for 2%

profile of v1, /device:TPU:65, one launch (start us, length us, event | category | flops | bytes accessed | tf_op | source)
XLA Modules:
  0.0 237.7 jit_solution(13956490763511107069)
XLA Ops:
  0.0 0.7 reduce
  0.8 0.8 fusion.6
  1.6 64.2 %all-gather = bf16[576,640]{1,0:T(8,128)(2,1)S(1)} all-gather(bf16[72,640]{1,0:T(8,128)(2,1)S(1)} %fusion.6), channel_id=2, replica_groups=mesh['group'=2,'x'=8,'zh'=4,'zm'=2,'zp'=2,'tp'=2] {'zh','zm'}, dimensions={0}, use_global_device_ids=true | all-gather | bytes 829440 | tf_op jit(solution)/shard_map/all_gather | solution.py:362
  65.8 2.2 copy-done.1
  68.0 3.9 %split_columns.1 = (bf16[256,4096]{1,0:T(8,128)(2,1)S(1)}, bf16[256,4096]{1,0:T(8,128)(2,1)}) custom-call(s32[1]{0:T(128)} %bitcast.2.p_ref, bf16[256,8192]{1,0:T(8,128)(2,1)S(1)} %copy-done.1), custom_call_target="tpu_custom_call" | custom-call | tf_op jit(solution)/shard_map/split_columns/pallas_call | solution.py:71
  71.9 1.3 copy-done.2
  73.3 2.6 %collective-permute-start.14 = (bf16[256,4096]{1,0:T(8,128)(2,1)}, bf16[256,4096]{1,0:T(8,128)(2,1)}, u32[]{:S(2)}, u32[]{:S(2)}) collective-permute-start(bf16[256,4096]{1,0:T(8,128)(2,1)} %get-tuple-element.10), channel_id=1, source_target_pairs={{0,2},{2,0},{1,3},{3,1},{4,6},{6,4},{5,7},{7,5},{8,10},{10,8},{9,1... | collective-permute-start | bytes 6291464 | tf_op jit(solution)/shard_map/ppermute | solution.py:44
  76.0 4.9 %collective-permute-start = (bf16[272,640]{1,0:T(8,128)(2,1)S(1)}, bf16[272,640]{1,0:T(8,128)(2,1)S(1)}, u32[]{:S(2)}, u32[]{:S(2)}) collective-permute-start(bf16[272,640]{1,0:T(8,128)(2,1)S(1)} %pad_maximum_fusion.refs_0_), channel_id=1, source_target_pairs={{0,32},{32,64},{64,96},{96,128},{128,160},{160,192},{192,224},{224... | collective-permute-start | bytes 1044488 | tf_op jit(solution)/shard_map/ppermute | solution.py:40
  81.0 4.1 %collective-permute-start.3 = (bf16[272,640]{1,0:T(8,128)(2,1)S(1)}, bf16[272,640]{1,0:T(8,128)(2,1)S(1)}, u32[]{:S(2)}, u32[]{:S(2)}) collective-permute-start(bf16[272,640]{1,0:T(8,128)(2,1)S(1)} %pad_maximum_fusion.1.refs_1_), channel_id=1, source_target_pairs={{0,224},{32,0},{64,32},{96,64},{128,96},{160,128},{192,160},{224,1... | collective-permute-start | bytes 1044488 | tf_op jit(solution)/shard_map/ppermute | solution.py:40
  85.1 2.0 collective-permute-start.1
  87.1 4.6 %collective-permute-start.2 = (bf16[272,640]{1,0:T(8,128)(2,1)S(1)}, bf16[272,640]{1,0:T(8,128)(2,1)S(1)}, u32[]{:S(2)}, u32[]{:S(2)}) collective-permute-start(bf16[272,640]{1,0:T(8,128)(2,1)S(1)} %pad_maximum_fusion.refs_0_), channel_id=1, source_target_pairs={{0,224},{32,0},{64,32},{96,64},{128,96},{160,128},{192,160},{224,1... | collective-permute-start | bytes 1044488 | tf_op jit(solution)/shard_map/ppermute | solution.py:40
  91.7 2.0 collective-permute-start.4
  93.7 4.6 %collective-permute-start.7 = (bf16[272,640]{1,0:T(8,128)(2,1)S(1)}, bf16[272,640]{1,0:T(8,128)(2,1)S(1)}, u32[]{:S(2)}, u32[]{:S(2)}) collective-permute-start(bf16[272,640]{1,0:T(8,128)(2,1)S(1)} %collective-permute-done.3.refs_5_.refs_3_), channel_id=1, source_target_pairs={{0,224},{32,0},{64,32},{96,64},{128,96},{160,128},{192,160},{224,1... | collective-permute-start | bytes 1044488 | tf_op jit(solution)/shard_map/ppermute | solution.py:40
  98.4 2.0 collective-permute-start.5
  100.4 4.6 %collective-permute-start.6 = (bf16[272,640]{1,0:T(8,128)(2,1)S(1)}, bf16[272,640]{1,0:T(8,128)(2,1)S(1)}, u32[]{:S(2)}, u32[]{:S(2)}) collective-permute-start(bf16[272,640]{1,0:T(8,128)(2,1)S(1)} %collective-permute-done.2.refs_4_.refs_2_), channel_id=1, source_target_pairs={{0,224},{32,0},{64,32},{96,64},{128,96},{160,128},{192,160},{224,1... | collective-permute-start | bytes 1044488 | tf_op jit(solution)/shard_map/ppermute | solution.py:40
  105.3 1.9 collective-permute-start.8
  107.3 5.0 %collective-permute-start.11 = (bf16[272,640]{1,0:T(8,128)(2,1)S(1)}, bf16[272,640]{1,0:T(8,128)(2,1)}, u32[]{:S(2)}, u32[]{:S(2)}) collective-permute-start(bf16[272,640]{1,0:T(8,128)(2,1)S(1)} %collective-permute-done.7.refs_9_.refs_5_), channel_id=1, source_target_pairs={{0,224},{32,0},{64,32},{96,64},{128,96},{160,128},{192,160},{224,1... | collective-permute-start | bytes 1044488 | tf_op jit(solution)/shard_map/ppermute | solution.py:40
  112.5 0.6 convert_reduce_fusion
  113.1 2.0 collective-permute-start.9
  115.1 4.6 %collective-permute-start.10 = (bf16[272,640]{1,0:T(8,128)(2,1)S(1)}, bf16[272,640]{1,0:T(8,128)(2,1)}, u32[]{:S(2)}, u32[]{:S(2)}) collective-permute-start(bf16[272,640]{1,0:T(8,128)(2,1)S(1)} %collective-permute-done.6.refs_8_.refs_4_), channel_id=1, source_target_pairs={{0,224},{32,0},{64,32},{96,64},{128,96},{160,128},{192,160},{224,1... | collective-permute-start | bytes 1044488 | tf_op jit(solution)/shard_map/ppermute | solution.py:40
  119.7 0.6 collective-permute-done.8.refs_10_
  120.4 1.9 collective-permute-start.12
  122.3 5.0 %collective-permute-start.13 = (bf16[272,640]{1,0:T(8,128)(2,1)}, bf16[272,640]{1,0:T(8,128)(2,1)}, u32[]{:S(2)}, u32[]{:S(2)}) collective-permute-start(bf16[272,640]{1,0:T(8,128)(2,1)} %collective-permute-done.11.refs_13_.refs_7_), channel_id=1, source_target_pairs={{0,224},{32,0},{64,32},{96,64},{128,96},{160,128},{192,160},{224,1... | collective-permute-start | bytes 1044488 | tf_op jit(solution)/shard_map/ppermute | solution.py:40
  127.8 1.5 collective-permute-done.10.refs_12_.refs_6_
  129.3 6.0 %collective-permute-done.12.refs_14_.refs_8_ = bf16[272,640]{1,0:T(8,128)(2,1)} collective-permute-done((bf16[272,640]{1,0:T(8,128)(2,1)}, bf16[272,640]{1,0:T(8,128)(2,1)}, u32[]{:S(2)}, u32[]{:S(2)}) %collective-permute-start.12) | collective-permute-done | bytes 348192 | tf_op jit(solution)/shard_map/ppermute | solution.py:40
  135.3 1.6 collective-permute-done.13.refs_15_.refs_9_
  136.9 4.7 %project.3.after_ref = bf16[256,640]{1,0:T(8,128)(2,1)} custom-call(s32[1]{0:T(128)} %bitcast.1.x_ref, bf16[256,4096]{1,0:T(8,128)(2,1)} %collective-permute-done.14.a_ref, bf16[272,640]{1,0:T(8,128)(2,1)S(1)} %pad_maximum_fusion.refs_0_, bf16[272,640]{1,0:T(8,128)(2,1)S(1)} %pad_maximum_fusion.1.refs_1_, ...), custom_call_target="tpu_custom_call" | custom-call | tf_op jit(solution)/shard_map/project/pallas_call | solution.py:101
  141.6 1.9 collective-permute-start.15
  143.5 1.6 collect_tails.1.q0_ref
  145.1 3.4 %collective-permute-start.16 = (bf16[256,512]{1,0:T(8,128)(2,1)}, bf16[256,512]{1,0:T(8,128)(2,1)}, u32[]{:S(2)}, u32[]{:S(2)}) collective-permute-start(bf16[256,512]{1,0:T(8,128)(2,1)} %collect_tails.1.q0_ref), channel_id=1, source_target_pairs={{0,2},{2,0},{1,3},{3,1},{4,6},{6,4},{5,7},{7,5},{8,10},{10,8},{9,1... | collective-permute-start | bytes 786440 | tf_op jit(solution)/shard_map/ppermute | solution.py:44
  148.5 1.3 fusion.7
  149.9 0.7 reshape.132.adapter_ref
  150.9 1.2 pad_maximum_fusion.2
  152.1 1.6 copy-done.3
  153.7 3.4 %project.2.base_ref = f32[256,640]{1,0:T(8,128)S(1)} custom-call(s32[1]{0:T(128)} %bitcast.1.x_ref, bf16[256,4096]{1,0:T(8,128)(2,1)S(1)} %copy-done.3, bf16[272,640]{1,0:T(8,128)(2,1)S(1)} %pad_maximum_fusion.refs_0_, bf16[272,640]{1,0:T(8,128)(2,1)S(1)} %pad_maximum_fusion.1.refs_1_, bf16[272,640]{1,0:T(8,128)(2,1)S(1)} %collective-permute-done.refs_2_.refs_14_, ...), custom_call_target="tpu_custom_call" | custom-call | tf_op jit(solution)/shard_map/project/pallas_call | solution.py:101
  157.2 5.7 %partial_attention.1 = bf16[256,1152]{1,0:T(8,128)(2,1)} custom-call(s32[2]{0:T(128)S(1)} %pad_add_fusion.s_ref, f32[256,640]{1,0:T(8,128)S(1)} %project.2.base_ref, bf16[256,640]{1,0:T(8,128)(2,1)} %collective-permute-done.15.other_ref, bf16[64,256]{1,0:T(8,128)(2,1)S(1)} %copy-done.7, bf16[64,256]{1,0:T(8,128)(2,1)S(1)} %copy-done.8, ...), custom_call_target="tpu_custom_call" | custom-call | tf_op jit(solution)/shard_map/partial_attention/pallas_call | solution.py:444
  162.8 8.1 %all-to-all-start = ((bf16[32,8,1152]{2,1,0:T(8,128)(2,1)}), bf16[32,8,1152]{2,1,0:T(8,128)(2,1)S(1)}, u32[]{:S(2)}, u32[]{:S(2)}) async-start(bf16[32,8,1152]{2,1,0:T(8,128)(2,1)} %bitcast.9), calls=%async_computation | async-start | bytes 1179648 | tf_op jit(solution)/shard_map/all_to_all | solution.py:455
  171.0 0.7 fusion.16
  171.7 0.6 iota_compare_fusion.3
  173.1 10.5 %all-to-all-done = bf16[32,8,1152]{2,1,0:T(8,128)(2,1)S(1)} async-done(((bf16[32,8,1152]{2,1,0:T(8,128)(2,1)}), bf16[32,8,1152]{2,1,0:T(8,128)(2,1)S(1)}, u32[]{:S(2)}, u32[]{:S(2)}) %all-to-all-start) | async-done | bytes 589856 | tf_op jit(solution)/shard_map/all_to_all | solution.py:455
  183.6 0.5 merge_near.1
  184.1 19.8 %all_to_all.20 = bf16[4,8,1152]{2,1,0:T(8,128)(2,1)S(1)} all-to-all(bf16[4,8,1152]{2,1,0:T(8,128)(2,1)S(1)} %bitcast.45), channel_id=1, replica_groups=mesh['group'=2,'x'=8,'zh'=4,'zm'=2,'zp'=2,'tp'=2] {'zh'}, dimensions={0} | all-to-all | bytes 147456 | tf_op jit(solution)/shard_map/all_to_all | solution.py:464
  203.9 1.1 merge_far.1
  205.0 7.6 %all-to-all-start.2 = ((bf16[32,8,1024]{2,1,0:T(8,128)(2,1)}), bf16[32,8,1024]{2,1,0:T(8,128)(2,1)S(1)}, u32[]{:S(2)}, u32[]{:S(2)}) async-start(bf16[32,8,1024]{2,1,0:T(8,128)(2,1)} %bitcast.17), calls=%async_computation.2 | async-start | bytes 1048576 | tf_op jit(solution)/shard_map/all_to_all | solution.py:473
  212.8 12.2 %all-to-all-done.2 = bf16[32,8,1024]{2,1,0:T(8,128)(2,1)S(1)} async-done(((bf16[32,8,1024]{2,1,0:T(8,128)(2,1)}), bf16[32,8,1024]{2,1,0:T(8,128)(2,1)S(1)}, u32[]{:S(2)}, u32[]{:S(2)}) %all-to-all-start.2) | async-done | bytes 524320 | tf_op jit(solution)/shard_map/all_to_all | solution.py:473
  225.0 0.8 output_rows.1
  225.8 11.2 %all_to_all.21 = f32[2,64,128]{2,1,0:T(8,128)S(1)} all-to-all(f32[2,64,128]{2,1,0:T(8,128)S(1)} %bitcast.47), channel_id=1, replica_groups=mesh['group'=2,'x'=8,'zh'=4,'zm'=2,'zp'=2,'tp'=2] {'tp'}, dimensions={0} | all-to-all | bytes 131072 | tf_op jit(solution)/shard_map/all_to_all | solution.py:487
  237.1 0.6 reduce_sum.59
  (73 shorter events, 2.6 us)
Async XLA Ops:
  0.0 172.3 %copy-start = (bf16[1,256]{1,0:T(2,128)(2,1)S(1)}, bf16[1,256]{1,0:T(2,128)(2,1)}, u32[]{:S(2)}) copy-start(bf16[1,256]{1,0:T(2,128)(2,1)} %param.27) | copy-start | bytes 1540
  65.8 2.2 copy-start.1
  71.9 1.3 copy-start.2
  73.2 25.1 %copy-start.12 = (s32[8192,1]{0,1:T(1,128)S(1)}, s32[8192,1]{0,1:T(1,128)}, u32[]{:S(2)}) copy-start(s32[8192,1]{0,1:T(1,128)} %param.24) | copy-start | bytes 98308
  73.2 39.1 %copy-start.9 = (s32[128]{0:T(128)S(1)}, s32[128]{0:T(128)}, u32[]{:S(2)}) copy-start(s32[128]{0:T(128)} %param.23) | copy-start | bytes 1540
  73.2 39.1 %copy-start.15 = (s32[128]{0:T(128)S(1)}, s32[128]{0:T(128)}, u32[]{:S(2)}) copy-start(s32[128]{0:T(128)} %param.25) | copy-start | bytes 1540
  73.3 63.6 %collective-permute-start.14 = (bf16[256,4096]{1,0:T(8,128)(2,1)}, bf16[256,4096]{1,0:T(8,128)(2,1)}, u32[]{:S(2)}, u32[]{:S(2)}) collective-permute-start(bf16[256,4096]{1,0:T(8,128)(2,1)} %get-tuple-element.10), channel_id=1, source_target_pairs={{0,2},{2,0},{1,3},{3,1},{4,6},{6,4},{5,7},{7,5},{8,10},{10,8},{9,1... | collective-permute-start | bytes 6291464 | tf_op jit(solution)/shard_map/ppermute | solution.py:44
  76.0 15.7 %collective-permute-start = (bf16[272,640]{1,0:T(8,128)(2,1)S(1)}, bf16[272,640]{1,0:T(8,128)(2,1)S(1)}, u32[]{:S(2)}, u32[]{:S(2)}) collective-permute-start(bf16[272,640]{1,0:T(8,128)(2,1)S(1)} %pad_maximum_fusion.refs_0_), channel_id=1, source_target_pairs={{0,32},{32,64},{64,96},{96,128},{128,160},{160,192},{192,224},{224... | collective-permute-start | bytes 1044488 | tf_op jit(solution)/shard_map/ppermute | solution.py:40
  81.0 12.7 %collective-permute-start.3 = (bf16[272,640]{1,0:T(8,128)(2,1)S(1)}, bf16[272,640]{1,0:T(8,128)(2,1)S(1)}, u32[]{:S(2)}, u32[]{:S(2)}) collective-permute-start(bf16[272,640]{1,0:T(8,128)(2,1)S(1)} %pad_maximum_fusion.1.refs_1_), channel_id=1, source_target_pairs={{0,224},{32,0},{64,32},{96,64},{128,96},{160,128},{192,160},{224,1... | collective-permute-start | bytes 1044488 | tf_op jit(solution)/shard_map/ppermute | solution.py:40
  85.1 13.3 %collective-permute-start.1 = (bf16[272,640]{1,0:T(8,128)(2,1)S(1)}, bf16[272,640]{1,0:T(8,128)(2,1)S(1)}, u32[]{:S(2)}, u32[]{:S(2)}) collective-permute-start(bf16[272,640]{1,0:T(8,128)(2,1)S(1)} %pad_maximum_fusion.1.refs_1_), channel_id=1, source_target_pairs={{0,32},{32,64},{64,96},{96,128},{128,160},{160,192},{192,224},{224... | collective-permute-start | bytes 1044488 | tf_op jit(solution)/shard_map/ppermute | solution.py:40
  87.1 13.3 %collective-permute-start.2 = (bf16[272,640]{1,0:T(8,128)(2,1)S(1)}, bf16[272,640]{1,0:T(8,128)(2,1)S(1)}, u32[]{:S(2)}, u32[]{:S(2)}) collective-permute-start(bf16[272,640]{1,0:T(8,128)(2,1)S(1)} %pad_maximum_fusion.refs_0_), channel_id=1, source_target_pairs={{0,224},{32,0},{64,32},{96,64},{128,96},{160,128},{192,160},{224,1... | collective-permute-start | bytes 1044488 | tf_op jit(solution)/shard_map/ppermute | solution.py:40
  91.7 13.6 %collective-permute-start.4 = (bf16[272,640]{1,0:T(8,128)(2,1)S(1)}, bf16[272,640]{1,0:T(8,128)(2,1)S(1)}, u32[]{:S(2)}, u32[]{:S(2)}) collective-permute-start(bf16[272,640]{1,0:T(8,128)(2,1)S(1)} %collective-permute-done.refs_2_.refs_14_), channel_id=1, source_target_pairs={{0,32},{32,64},{64,96},{96,128},{128,160},{160,192},{192,224},{224... | collective-permute-start | bytes 1044488 | tf_op jit(solution)/shard_map/ppermute | solution.py:40
  93.7 13.6 %collective-permute-start.7 = (bf16[272,640]{1,0:T(8,128)(2,1)S(1)}, bf16[272,640]{1,0:T(8,128)(2,1)S(1)}, u32[]{:S(2)}, u32[]{:S(2)}) collective-permute-start(bf16[272,640]{1,0:T(8,128)(2,1)S(1)} %collective-permute-done.3.refs_5_.refs_3_), channel_id=1, source_target_pairs={{0,224},{32,0},{64,32},{96,64},{128,96},{160,128},{192,160},{224,1... | collective-permute-start | bytes 1044488 | tf_op jit(solution)/shard_map/ppermute | solution.py:40
  98.4 14.7 %collective-permute-start.5 = (bf16[272,640]{1,0:T(8,128)(2,1)S(1)}, bf16[272,640]{1,0:T(8,128)(2,1)S(1)}, u32[]{:S(2)}, u32[]{:S(2)}) collective-permute-start(bf16[272,640]{1,0:T(8,128)(2,1)S(1)} %collective-permute-done.1.refs_3_.refs_15_), channel_id=1, source_target_pairs={{0,32},{32,64},{64,96},{96,128},{128,160},{160,192},{192,224},{224... | collective-permute-start | bytes 1044488 | tf_op jit(solution)/shard_map/ppermute | solution.py:40
  100.4 14.7 %collective-permute-start.6 = (bf16[272,640]{1,0:T(8,128)(2,1)S(1)}, bf16[272,640]{1,0:T(8,128)(2,1)S(1)}, u32[]{:S(2)}, u32[]{:S(2)}) collective-permute-start(bf16[272,640]{1,0:T(8,128)(2,1)S(1)} %collective-permute-done.2.refs_4_.refs_2_), channel_id=1, source_target_pairs={{0,224},{32,0},{64,32},{96,64},{128,96},{160,128},{192,160},{224,1... | collective-permute-start | bytes 1044488 | tf_op jit(solution)/shard_map/ppermute | solution.py:40
  105.3 15.0 %collective-permute-start.8 = (bf16[272,640]{1,0:T(8,128)(2,1)S(1)}, bf16[272,640]{1,0:T(8,128)(2,1)}, u32[]{:S(2)}, u32[]{:S(2)}) collective-permute-start(bf16[272,640]{1,0:T(8,128)(2,1)S(1)} %collective-permute-done.4.refs_6_.refs_12_), channel_id=1, source_target_pairs={{0,32},{32,64},{64,96},{96,128},{128,160},{160,192},{192,224},{224... | collective-permute-start | bytes 1044488 | tf_op jit(solution)/shard_map/ppermute | solution.py:40
  107.3 15.0 %collective-permute-start.11 = (bf16[272,640]{1,0:T(8,128)(2,1)S(1)}, bf16[272,640]{1,0:T(8,128)(2,1)}, u32[]{:S(2)}, u32[]{:S(2)}) collective-permute-start(bf16[272,640]{1,0:T(8,128)(2,1)S(1)} %collective-permute-done.7.refs_9_.refs_5_), channel_id=1, source_target_pairs={{0,224},{32,0},{64,32},{96,64},{128,96},{160,128},{192,160},{224,1... | collective-permute-start | bytes 1044488 | tf_op jit(solution)/shard_map/ppermute | solution.py:40
  113.1 14.7 %collective-permute-start.9 = (bf16[272,640]{1,0:T(8,128)(2,1)S(1)}, bf16[272,640]{1,0:T(8,128)(2,1)}, u32[]{:S(2)}, u32[]{:S(2)}) collective-permute-start(bf16[272,640]{1,0:T(8,128)(2,1)S(1)} %collective-permute-done.5.refs_7_.refs_13_), channel_id=1, source_target_pairs={{0,32},{32,64},{64,96},{96,128},{128,160},{160,192},{192,224},{224... | collective-permute-start | bytes 1044488 | tf_op jit(solution)/shard_map/ppermute | solution.py:40
  115.1 14.2 %collective-permute-start.10 = (bf16[272,640]{1,0:T(8,128)(2,1)S(1)}, bf16[272,640]{1,0:T(8,128)(2,1)}, u32[]{:S(2)}, u32[]{:S(2)}) collective-permute-start(bf16[272,640]{1,0:T(8,128)(2,1)S(1)} %collective-permute-done.6.refs_8_.refs_4_), channel_id=1, source_target_pairs={{0,224},{32,0},{64,32},{96,64},{128,96},{160,128},{192,160},{224,1... | collective-permute-start | bytes 1044488 | tf_op jit(solution)/shard_map/ppermute | solution.py:40
  120.4 14.9 %collective-permute-start.12 = (bf16[272,640]{1,0:T(8,128)(2,1)}, bf16[272,640]{1,0:T(8,128)(2,1)}, u32[]{:S(2)}, u32[]{:S(2)}) collective-permute-start(bf16[272,640]{1,0:T(8,128)(2,1)} %collective-permute-done.8.refs_10_), channel_id=1, source_target_pairs={{0,32},{32,64},{64,96},{96,128},{128,160},{160,192},{192,224},{224... | collective-permute-start | bytes 1044488 | tf_op jit(solution)/shard_map/ppermute | solution.py:40
  122.3 14.6 %collective-permute-start.13 = (bf16[272,640]{1,0:T(8,128)(2,1)}, bf16[272,640]{1,0:T(8,128)(2,1)}, u32[]{:S(2)}, u32[]{:S(2)}) collective-permute-start(bf16[272,640]{1,0:T(8,128)(2,1)} %collective-permute-done.11.refs_13_.refs_7_), channel_id=1, source_target_pairs={{0,224},{32,0},{64,32},{96,64},{128,96},{160,128},{192,160},{224,1... | collective-permute-start | bytes 1044488 | tf_op jit(solution)/shard_map/ppermute | solution.py:40
  141.6 15.5 %collective-permute-start.15 = (bf16[256,640]{1,0:T(8,128)(2,1)}, bf16[256,640]{1,0:T(8,128)(2,1)}, u32[]{:S(2)}, u32[]{:S(2)}) collective-permute-start(bf16[256,640]{1,0:T(8,128)(2,1)} %project.3.after_ref), channel_id=1, source_target_pairs={{0,2},{2,0},{1,3},{3,1},{4,6},{6,4},{5,7},{7,5},{8,10},{10,8},{9,1... | collective-permute-start | bytes 983048 | tf_op jit(solution)/shard_map/ppermute | solution.py:44
  145.1 12.0 %collective-permute-start.16 = (bf16[256,512]{1,0:T(8,128)(2,1)}, bf16[256,512]{1,0:T(8,128)(2,1)}, u32[]{:S(2)}, u32[]{:S(2)}) collective-permute-start(bf16[256,512]{1,0:T(8,128)(2,1)} %collect_tails.1.q0_ref), channel_id=1, source_target_pairs={{0,2},{2,0},{1,3},{3,1},{4,6},{6,4},{5,7},{7,5},{8,10},{10,8},{9,1... | collective-permute-start | bytes 786440 | tf_op jit(solution)/shard_map/ppermute | solution.py:44
  152.1 1.6 copy-start.3
  153.7 3.4 %copy-start.4 = (s32[256,1]{1,0:T(8,128)S(1)}, s32[256,1]{1,0:T(8,128)}, u32[]{:S(2)}) copy-start(s32[256,1]{1,0:T(8,128)} %reshape.132.adapter_ref) | copy-start | bytes 3076
  153.7 3.4 %copy-start.7 = (bf16[64,256]{1,0:T(8,128)(2,1)S(1)}, bf16[64,256]{1,0:T(8,128)(2,1)}, u32[]{:S(2)}) copy-start(bf16[64,256]{1,0:T(8,128)(2,1)} %upk_ref.1) | copy-start | bytes 98308
  153.7 3.4 %copy-start.8 = (bf16[64,256]{1,0:T(8,128)(2,1)S(1)}, bf16[64,256]{1,0:T(8,128)(2,1)}, u32[]{:S(2)}) copy-start(bf16[64,256]{1,0:T(8,128)(2,1)} %upv_ref.1) | copy-start | bytes 98308
  157.1 13.8 %copy-start.10 = (bf16[1,256,256]{2,1,0:T(8,128)(2,1)S(1)}, bf16[1,256,256]{2,1,0:T(8,128)(2,1)}, u32[]{:S(2)}) copy-start(bf16[1,256,256]{2,1,0:T(8,128)(2,1)} %param.30) | copy-start | bytes 393220
  157.1 13.9 %copy-start.11 = (bf16[1,256,256]{2,1,0:T(8,128)(2,1)S(1)}, bf16[1,256,256]{2,1,0:T(8,128)(2,1)}, u32[]{:S(2)}) copy-start(bf16[1,256,256]{2,1,0:T(8,128)(2,1)} %param.29) | copy-start | bytes 393220
  157.2 13.9 %copy-start.14 = (bf16[1,256]{1,0:T(2,128)(2,1)S(1)}, bf16[1,256]{1,0:T(2,128)(2,1)}, u32[]{:S(2)}) copy-start(bf16[1,256]{1,0:T(2,128)(2,1)} %param.28) | copy-start | bytes 1540
  162.8 49.8 %copy-start.13 = (bf16[64,64]{1,0:T(8,128)(2,1)S(1)}, bf16[64,64]{1,0:T(8,128)(2,1)}, u32[]{:S(2)}) copy-start(bf16[64,64]{1,0:T(8,128)(2,1)} %param.33) | copy-start | bytes 24580
  162.8 62.2 %copy-start.5 = (bf16[2048,64]{0,1:T(8,128)(2,1)S(1)}, bf16[2048,64]{0,1:T(8,128)(2,1)}, u32[]{:S(2)}) copy-start(bf16[2048,64]{0,1:T(8,128)(2,1)} %param.31) | copy-start | bytes 786436
  162.8 62.2 %copy-start.6 = (bf16[2048,64]{0,1:T(8,128)(2,1)S(1)}, bf16[2048,64]{0,1:T(8,128)(2,1)}, u32[]{:S(2)}) copy-start(bf16[2048,64]{0,1:T(8,128)(2,1)} %param.32) | copy-start | bytes 786436
  162.8 20.8 %all-to-all-start = ((bf16[32,8,1152]{2,1,0:T(8,128)(2,1)}), bf16[32,8,1152]{2,1,0:T(8,128)(2,1)S(1)}, u32[]{:S(2)}, u32[]{:S(2)}) async-start(bf16[32,8,1152]{2,1,0:T(8,128)(2,1)} %bitcast.9), calls=%async_computation | async-start | bytes 1179648 | tf_op jit(solution)/shard_map/all_to_all | solution.py:455
  205.0 20.0 %all-to-all-start.2 = ((bf16[32,8,1024]{2,1,0:T(8,128)(2,1)}), bf16[32,8,1024]{2,1,0:T(8,128)(2,1)S(1)}, u32[]{:S(2)}, u32[]{:S(2)}) async-start(bf16[32,8,1024]{2,1,0:T(8,128)(2,1)} %bitcast.17), calls=%async_computation.2 | async-start | bytes 1048576 | tf_op jit(solution)/shard_map/all_to_all | solution.py:473

commit v2 on v1

--- a/solution.py
+++ b/solution.py
@@ -74,7 +74,7 @@
         in_specs=[SMEM, pl.BlockSpec((block, width), lambda i: (i, 0))],
         out_specs=[pl.BlockSpec((block, width // 2), lambda i: (i, 0))] * 2,
         out_shape=[out, out],
-        compiler_params=room(8),
+        compiler_params=room(58),
         name="split_columns",
     )(parity, act)
 
@@ -166,55 +166,64 @@
         spun = part * cos_ref[...] + pltpu.roll(part, HEAD // 2, 1) * sin_ref[...]
         turned.append(spun.astype(bf16))
     source = q0_ref.shape[0]
+    half_rows = rows // kv
     blocks = 4
-    i = lax.broadcasted_iota(jnp.int32, (rows, source), 1)
-    row = lax.broadcasted_iota(jnp.int32, (rows, source), 0)
-    row_half = lax.rem(row // NZH, 2)
-    row_base = row - row_half * NZH
+    i = lax.broadcasted_iota(jnp.int32, (half_rows, source), 1)
+    row = lax.broadcasted_iota(jnp.int32, (half_rows, source), 0)
     block = lax.rem(i, blocks)
     z8 = lax.rem(i // blocks, NZH * NZM)
     off = i // (blocks * NZH * NZM)
     xs = lax.rem(off + me, NX)
-    spot = (xs * (NZM * NZP) + lax.rem(z8, NZM) * NZP) * (2 * NZH) + z8 // NZM
-    hit0 = row_base == spot + parity * (2 * NZH)
-    hit1 = row_base == spot + (1 - parity) * (2 * NZH)
-    queries = []
-    for g in range(2):
-        right = block == 2 * row_half + g
-        pick0 = jnp.where(hit0 & right, 1.0, 0.0).astype(bf16)
-        pick1 = jnp.where(hit1 & right, 1.0, 0.0).astype(bf16)
-        got = jnp.dot(pick0, q0_ref[...], preferred_element_type=f32) + jnp.dot(
-            pick1, q1_ref[...], preferred_element_type=f32
-        )
-        queries.append(got.astype(bf16))
-    t_row = lax.broadcasted_iota(jnp.int32, (rows, tokens), 0)
-    t_first = lax.rem(t_row // NZH, 2) == 0
-    mask = t_row - jnp.where(t_first, 0, NZH) == owner_ref[...]
-    lane = lax.broadcasted_iota(jnp.int32, (rows, HEAD), 1)
-    stat = jnp.zeros((rows, HEAD), f32)
+    spot = (xs * (NZM * NZP) + lax.rem(z8, NZM) * NZP) * NZH + z8 // NZM
+    hit0 = row == spot + parity * NZH
+    hit1 = row == spot + (1 - parity) * NZH
+    mask = lax.broadcasted_iota(jnp.int32, (half_rows, tokens), 0) == owner_ref[...]
+    lane = lax.broadcasted_iota(jnp.int32, (half_rows, HEAD), 1)
     across = (((1,), (1,)), ((), ()))
-    for h in range(heads):
-        q = queries[h // 4][:, (h % 4) * HEAD : (h % 4 + 1) * HEAD]
-        s0 = lax.dot_general(q, turned[0], across, preferred_element_type=f32)
-        s1 = lax.dot_general(q, turned[1], across, preferred_element_type=f32)
-        s = jnp.where(mask, jnp.where(t_first, s0, s1) * (HEAD ** (-0.5)), NEG)
-        top = jnp.max(s, axis=1, keepdims=True)
-        e = jnp.where(mask, jnp.exp(s - top), 0.0)
-        total = jnp.sum(e, axis=1, keepdims=True)
-        e0 = jnp.where(t_first, e, 0.0).astype(bf16)
-        e1 = jnp.where(t_first, 0.0, e).astype(bf16)
-        o = jnp.dot(e0, value[:, :HEAD], preferred_element_type=f32) + jnp.dot(
-            e1, value[:, HEAD:], preferred_element_type=f32
-        )
-        full = total > 0.0
-        o = o * jnp.where(full, 1.0 / jnp.maximum(total, 1e-30), 0.0)
-        out_ref[:, h * HEAD : (h + 1) * HEAD] = o.astype(bf16)
-        lse = jnp.where(full, top + jnp.log(jnp.maximum(total, 1e-30)), NEG)
-        hi, mid, lo = three_terms(lse)
-        stat = jnp.where(lane == h, hi, stat)
-        stat = jnp.where(lane == heads + h, mid, stat)
-        stat = jnp.where(lane == 2 * heads + h, lo, stat)
-    out_ref[:, heads * HEAD :] = stat.astype(bf16)
+    outs = [[] for _ in range(kv)]
+    for k in range(kv):
+        stat = jnp.zeros((half_rows, HEAD), f32)
+        for g in range(blocks // kv):
+            right = block == k * (blocks // kv) + g
+            pick0 = jnp.where(hit0 & right, 1.0, 0.0).astype(bf16)
+            pick1 = jnp.where(hit1 & right, 1.0, 0.0).astype(bf16)
+            got = jnp.dot(pick0, q0_ref[...], preferred_element_type=f32) + jnp.dot(
+                pick1, q1_ref[...], preferred_element_type=f32
+            )
+            got = got.astype(bf16)
+            for j in range(got.shape[1] // HEAD):
+                h = g * (got.shape[1] // HEAD) + j
+                q = got[:, j * HEAD : (j + 1) * HEAD]
+                s = lax.dot_general(q, turned[k], across, preferred_element_type=f32)
+                s = jnp.where(mask, s * (HEAD ** (-0.5)), NEG)
+                top = jnp.max(s, axis=1, keepdims=True)
+                e = jnp.where(mask, jnp.exp(s - top), 0.0)
+                total = jnp.sum(e, axis=1, keepdims=True)
+                o = jnp.dot(
+                    e.astype(bf16), value[:, k * HEAD : (k + 1) * HEAD],
+                    preferred_element_type=f32,
+                )
+                full = total > 0.0
+                o = o * jnp.where(full, 1.0 / jnp.maximum(total, 1e-30), 0.0)
+                outs[k].append(o.astype(bf16))
+                lse = jnp.where(full, top + jnp.log(jnp.maximum(total, 1e-30)), NEG)
+                hi, mid, lo = three_terms(lse)
+                stat = jnp.where(lane == h, hi, stat)
+                stat = jnp.where(lane == heads + h, mid, stat)
+                stat = jnp.where(lane == 2 * heads + h, lo, stat)
+        outs[k].append(stat.astype(bf16))
+    to = lax.broadcasted_iota(jnp.int32, (rows, half_rows), 0)
+    come = lax.broadcasted_iota(jnp.int32, (rows, half_rows), 1)
+    unit = kv * NZH
+    place = (come // NZH) * unit + lax.rem(come, NZH)
+    moves = [
+        jnp.where(to == place + k * NZH, 1.0, 0.0).astype(bf16) for k in range(kv)
+    ]
+    for h in range(heads + 1):
+        moved = jnp.dot(moves[0], outs[0][h], preferred_element_type=f32)
+        for k in range(1, kv):
+            moved = moved + jnp.dot(moves[k], outs[k][h], preferred_element_type=f32)
+        out_ref[:, h * HEAD : (h + 1) * HEAD] = moved.astype(bf16)
 
 
 def reduce_rows(v, op):
@@ -377,8 +386,7 @@
         )
     chunk_depth = per_chunk * depth
 
-    activations, _ = lax.optimization_barrier((prompt_activations, column))
-    mine, theirs = split_columns(activations, parity[None])
+    mine, theirs = split_columns(prompt_activations, parity[None])
     partner_act = swap_pair(theirs)
 
     by_offset = {0: pieces}
@@ -414,7 +422,7 @@
     near = NZH * NZM * NZP
     z = my_owners % near
     z_low = z % (NZM * NZP)
-    owner_spot = ((my_owners // near) * (NZM * NZP) + z_low) * (2 * NZH) + z // (NZM * NZP)
+    owner_spot = ((my_owners // near) * (NZM * NZP) + z_low) * NZH + z // (NZM * NZP)
     inside = jnp.arange(PAGE, dtype=jnp.int32)[None, :]
     position = ((start + rank * PAGE)[:, None] + inside).reshape(-1)
     token_adapter = jnp.broadcast_to(adapter[:, None], (pages, PAGE)).reshape(-1, 1)

time: 239 us -> 277 us (1.16)
  blocking collectives: 95.2 us -> 131 us
  starting transfers between devices: 72.8 us -> 76.5 us
  local copies, waits for them, and re-layouts: 6.55 us -> 3.06 us
  Pallas kernels: 21.7 us -> 24.5 us
    all_gather x1, blocking collectives: 64.2 us -> 105 us  [per_device(): column = lax.all_gather(block, Z8)]
    ppermute x3, starting transfers between devices: 7.95 us -> 12 us  [swap_pair(): return lax.ppermute(x, 'zp', [(0, 1), (1, 0)])]
    unnamed x34 -> x38, local copies, waits for them, and re-layouts: 5.25 us -> 1.75 us
    pallas_call x1, Pallas kernels: 3.92 us -> 7.35 us  [split_columns(): pl.pallas_call(split_kernel, grid=(rows // block,), in_specs=[SMEM, pl.Bl...]
    all_to_all x1, blocking collectives: 11.2 us -> 8.11 us  [per_device(): lax.all_to_all(partial_output.reshape(pair, columns, requests), 'tp', 0,...]
where the time goes in v2:
time: 277 us; the launch traced here: 276 us
  blocking collectives  131 us (47%)
  starting transfers between devices  76.5 us (28%)
  waiting for transfers between devices  34.1 us (12%)
  Pallas kernels  24.5 us (9%)
  other arithmetic  5.69 us (2%)
  local copies, waits for them, and re-layouts  3.06 us (1%)
    all_gather x1, blocking collectives, per_device(): column = lax.all_gather(block, Z8)  105 us
    ppermute x14, starting transfers between devices, ring_x(): return lax.ppermute(x, 'x', [(i, (i + step) % NX) for i in range(NX)])  46.7 us
    all_to_all x1, blocking collectives, per_device(): lax.all_to_all(merged.reshape(NZH, unit, full_width), 'zh', 0, 0, tiled=T...  18 us
    all_to_all x1, waiting for transfers between devices, per_device(): lax.all_to_all(mixed.reshape(members, unit, half_width), NEAR, 0, 0, tile...  12.8 us
    ppermute x3, starting transfers between devices, swap_pair(): return lax.ppermute(x, 'zp', [(0, 1), (1, 0)])  12 us
    all_to_all x1, waiting for transfers between devices, per_device(): lax.all_to_all(payload.reshape(members, unit, full_width), NEAR, 0, 0, ti...  10.8 us
    ppermute x14, waiting for transfers between devices, ring_x(): return lax.ppermute(x, 'x', [(i, (i + step) % NX) for i in range(NX)])  10.4 us
    all_to_all x1, starting transfers between devices, per_device(): lax.all_to_all(mixed.reshape(members, unit, half_width), NEAR, 0, 0, tile...  9.2 us
  transfers between devices with their start and end apart: 19, of which 8 were waited for; matrix products, arithmetic and copies ran while one was open for 3% of the time, Pallas kernels for 2%

profile of v2, /device:TPU:65, one launch (start us, length us, event | category | flops | bytes accessed | tf_op | source)
XLA Modules:
  0.0 275.7 jit_solution(11988014932193080162)
XLA Ops:
  0.0 7.4 %split_columns.1 = (bf16[256,4096]{1,0:T(8,128)(2,1)}, bf16[256,4096]{1,0:T(8,128)(2,1)}) custom-call(s32[1]{0:T(128)} %bitcast.2.p_ref, bf16[256,8192]{1,0:T(8,128)(2,1)} %a_ref.1), custom_call_target="tpu_custom_call" | custom-call | tf_op jit(solution)/shard_map/split_columns/pallas_call | solution.py:71
  7.4 6.7 %collective-permute-start.14 = (bf16[256,4096]{1,0:T(8,128)(2,1)}, bf16[256,4096]{1,0:T(8,128)(2,1)}, u32[]{:S(2)}, u32[]{:S(2)}) collective-permute-start(bf16[256,4096]{1,0:T(8,128)(2,1)} %get-tuple-element.8), channel_id=1, source_target_pairs={{0,2},{2,0},{1,3},{3,1},{4,6},{6,4},{5,7},{7,5},{8,10},{10,8},{9,1... | collective-permute-start | bytes 6291464 | tf_op jit(solution)/shard_map/ppermute | solution.py:44
  14.2 104.7 %all-gather = bf16[576,640]{1,0:T(8,128)(2,1)S(1)} all-gather(bf16[72,640]{1,0:T(8,128)(2,1)S(1)} %fusion.6), channel_id=2, replica_groups=mesh['group'=2,'x'=8,'zh'=4,'zm'=2,'zp'=2,'tp'=2] {'zh','zm'}, dimensions={0}, use_global_device_ids=true | all-gather | bytes 829440 | tf_op jit(solution)/shard_map/all_gather | solution.py:371
  119.0 3.3 %collective-permute-start = (bf16[272,640]{1,0:T(8,128)(2,1)S(1)}, bf16[272,640]{1,0:T(8,128)(2,1)S(1)}, u32[]{:S(2)}, u32[]{:S(2)}) collective-permute-start(bf16[272,640]{1,0:T(8,128)(2,1)S(1)} %pad_maximum_fusion.refs_0_), channel_id=1, source_target_pairs={{0,32},{32,64},{64,96},{96,128},{128,160},{160,192},{192,224},{224... | collective-permute-start | bytes 1044488 | tf_op jit(solution)/shard_map/ppermute | solution.py:40
  122.4 4.1 %collective-permute-start.3 = (bf16[272,640]{1,0:T(8,128)(2,1)S(1)}, bf16[272,640]{1,0:T(8,128)(2,1)S(1)}, u32[]{:S(2)}, u32[]{:S(2)}) collective-permute-start(bf16[272,640]{1,0:T(8,128)(2,1)S(1)} %pad_maximum_fusion.1.refs_1_), channel_id=1, source_target_pairs={{0,224},{32,0},{64,32},{96,64},{128,96},{160,128},{192,160},{224,1... | collective-permute-start | bytes 1044488 | tf_op jit(solution)/shard_map/ppermute | solution.py:40
  126.5 2.0 collective-permute-start.1
  128.5 4.6 %collective-permute-start.2 = (bf16[272,640]{1,0:T(8,128)(2,1)S(1)}, bf16[272,640]{1,0:T(8,128)(2,1)S(1)}, u32[]{:S(2)}, u32[]{:S(2)}) collective-permute-start(bf16[272,640]{1,0:T(8,128)(2,1)S(1)} %pad_maximum_fusion.refs_0_), channel_id=1, source_target_pairs={{0,224},{32,0},{64,32},{96,64},{128,96},{160,128},{192,160},{224,1... | collective-permute-start | bytes 1044488 | tf_op jit(solution)/shard_map/ppermute | solution.py:40
  133.1 2.0 collective-permute-start.4
  135.1 4.6 %collective-permute-start.7 = (bf16[272,640]{1,0:T(8,128)(2,1)S(1)}, bf16[272,640]{1,0:T(8,128)(2,1)S(1)}, u32[]{:S(2)}, u32[]{:S(2)}) collective-permute-start(bf16[272,640]{1,0:T(8,128)(2,1)S(1)} %collective-permute-done.3.refs_5_.refs_3_), channel_id=1, source_target_pairs={{0,224},{32,0},{64,32},{96,64},{128,96},{160,128},{192,160},{224,1... | collective-permute-start | bytes 1044488 | tf_op jit(solution)/shard_map/ppermute | solution.py:40
  139.8 2.0 collective-permute-start.5
  141.8 4.6 %collective-permute-start.6 = (bf16[272,640]{1,0:T(8,128)(2,1)S(1)}, bf16[272,640]{1,0:T(8,128)(2,1)S(1)}, u32[]{:S(2)}, u32[]{:S(2)}) collective-permute-start(bf16[272,640]{1,0:T(8,128)(2,1)S(1)} %collective-permute-done.2.refs_4_.refs_2_), channel_id=1, source_target_pairs={{0,224},{32,0},{64,32},{96,64},{128,96},{160,128},{192,160},{224,1... | collective-permute-start | bytes 1044488 | tf_op jit(solution)/shard_map/ppermute | solution.py:40
  146.4 0.4 collective-permute-done.4.refs_6_.refs_12_
  146.8 1.9 collective-permute-start.8
  148.7 4.6 %collective-permute-start.11 = (bf16[272,640]{1,0:T(8,128)(2,1)S(1)}, bf16[272,640]{1,0:T(8,128)(2,1)}, u32[]{:S(2)}, u32[]{:S(2)}) collective-permute-start(bf16[272,640]{1,0:T(8,128)(2,1)S(1)} %collective-permute-done.7.refs_9_.refs_5_), channel_id=1, source_target_pairs={{0,224},{32,0},{64,32},{96,64},{128,96},{160,128},{192,160},{224,1... | collective-permute-start | bytes 1044488 | tf_op jit(solution)/shard_map/ppermute | solution.py:40
  153.6 0.6 convert_reduce_fusion
  154.2 1.9 collective-permute-start.9
  156.2 4.6 %collective-permute-start.10 = (bf16[272,640]{1,0:T(8,128)(2,1)S(1)}, bf16[272,640]{1,0:T(8,128)(2,1)}, u32[]{:S(2)}, u32[]{:S(2)}) collective-permute-start(bf16[272,640]{1,0:T(8,128)(2,1)S(1)} %collective-permute-done.6.refs_8_.refs_4_), channel_id=1, source_target_pairs={{0,224},{32,0},{64,32},{96,64},{128,96},{160,128},{192,160},{224,1... | collective-permute-start | bytes 1044488 | tf_op jit(solution)/shard_map/ppermute | solution.py:40
  160.8 0.9 collective-permute-done.8.refs_10_
  161.7 1.9 collective-permute-start.12
  163.7 4.6 %collective-permute-start.13 = (bf16[272,640]{1,0:T(8,128)(2,1)}, bf16[272,640]{1,0:T(8,128)(2,1)}, u32[]{:S(2)}, u32[]{:S(2)}) collective-permute-start(bf16[272,640]{1,0:T(8,128)(2,1)} %collective-permute-done.11.refs_13_.refs_7_), channel_id=1, source_target_pairs={{0,224},{32,0},{64,32},{96,64},{128,96},{160,128},{192,160},{224,1... | collective-permute-start | bytes 1044488 | tf_op jit(solution)/shard_map/ppermute | solution.py:40
  168.5 0.8 collective-permute-done.9.refs_11_
  169.3 0.8 collective-permute-done.10.refs_12_.refs_6_
  170.0 6.7 %collective-permute-done.12.refs_14_.refs_8_ = bf16[272,640]{1,0:T(8,128)(2,1)} collective-permute-done((bf16[272,640]{1,0:T(8,128)(2,1)}, bf16[272,640]{1,0:T(8,128)(2,1)}, u32[]{:S(2)}, u32[]{:S(2)}) %collective-permute-start.12) | collective-permute-done | bytes 348192 | tf_op jit(solution)/shard_map/ppermute | solution.py:40
  176.7 0.9 collective-permute-done.13.refs_15_.refs_9_
  177.6 4.7 %project.3.after_ref = bf16[256,640]{1,0:T(8,128)(2,1)} custom-call(s32[1]{0:T(128)} %bitcast.1.x_ref, bf16[256,4096]{1,0:T(8,128)(2,1)} %collective-permute-done.14.a_ref, bf16[272,640]{1,0:T(8,128)(2,1)S(1)} %pad_maximum_fusion.refs_0_, bf16[272,640]{1,0:T(8,128)(2,1)S(1)} %pad_maximum_fusion.1.refs_1_, ...), custom_call_target="tpu_custom_call" | custom-call | tf_op jit(solution)/shard_map/project/pallas_call | solution.py:101
  182.3 1.9 collective-permute-start.15
  184.3 1.6 collect_tails.1.q0_ref
  185.8 3.4 %collective-permute-start.16 = (bf16[256,512]{1,0:T(8,128)(2,1)}, bf16[256,512]{1,0:T(8,128)(2,1)}, u32[]{:S(2)}, u32[]{:S(2)}) collective-permute-start(bf16[256,512]{1,0:T(8,128)(2,1)} %collect_tails.1.q0_ref), channel_id=1, source_target_pairs={{0,2},{2,0},{1,3},{3,1},{4,6},{6,4},{5,7},{7,5},{8,10},{10,8},{9,1... | collective-permute-start | bytes 786440 | tf_op jit(solution)/shard_map/ppermute | solution.py:44
  189.2 1.3 fusion.7
  190.6 0.8 reshape.132.adapter_ref
  191.6 1.2 pad_maximum_fusion.2
  192.8 1.6 copy-done.1
  194.4 3.4 %project.2.base_ref = f32[256,640]{1,0:T(8,128)S(1)} custom-call(s32[1]{0:T(128)} %bitcast.1.x_ref, bf16[256,4096]{1,0:T(8,128)(2,1)S(1)} %copy-done.1, bf16[272,640]{1,0:T(8,128)(2,1)S(1)} %pad_maximum_fusion.refs_0_, bf16[272,640]{1,0:T(8,128)(2,1)S(1)} %pad_maximum_fusion.1.refs_1_, bf16[272,640]{1,0:T(8,128)(2,1)S(1)} %collective-permute-done.refs_2_.refs_14_, ...), custom_call_target="tpu_custom_call" | custom-call | tf_op jit(solution)/shard_map/project/pallas_call | solution.py:101
  197.9 5.0 %partial_attention.1 = bf16[256,1152]{1,0:T(8,128)(2,1)} custom-call(s32[2]{0:T(128)S(1)} %pad_add_fusion.s_ref, f32[256,640]{1,0:T(8,128)S(1)} %project.2.base_ref, bf16[256,640]{1,0:T(8,128)(2,1)} %collective-permute-done.15.other_ref, bf16[64,256]{1,0:T(8,128)(2,1)S(1)} %copy-done.5, bf16[64,256]{1,0:T(8,128)(2,1)S(1)} %copy-done.6, ...), custom_call_target="tpu_custom_call" | custom-call | tf_op jit(solution)/shard_map/partial_attention/pallas_call | solution.py:452
  202.9 8.6 %all-to-all-start = ((bf16[32,8,1152]{2,1,0:T(8,128)(2,1)}), bf16[32,8,1152]{2,1,0:T(8,128)(2,1)S(1)}, u32[]{:S(2)}, u32[]{:S(2)}) async-start(bf16[32,8,1152]{2,1,0:T(8,128)(2,1)} %bitcast.9), calls=%async_computation | async-start | bytes 1179648 | tf_op jit(solution)/shard_map/all_to_all | solution.py:463
  211.6 0.6 fusion.16
  212.2 0.6 iota_compare_fusion.3
  212.9 0.2 fusion.23
  213.3 0.2 fusion.2
  213.5 10.8 %all-to-all-done = bf16[32,8,1152]{2,1,0:T(8,128)(2,1)S(1)} async-done(((bf16[32,8,1152]{2,1,0:T(8,128)(2,1)}), bf16[32,8,1152]{2,1,0:T(8,128)(2,1)S(1)}, u32[]{:S(2)}, u32[]{:S(2)}) %all-to-all-start) | async-done | bytes 589856 | tf_op jit(solution)/shard_map/all_to_all | solution.py:463
  224.3 0.5 merge_near.1
  224.8 18.0 %all_to_all.20 = bf16[4,8,1152]{2,1,0:T(8,128)(2,1)S(1)} all-to-all(bf16[4,8,1152]{2,1,0:T(8,128)(2,1)S(1)} %bitcast.45), channel_id=1, replica_groups=mesh['group'=2,'x'=8,'zh'=4,'zm'=2,'zp'=2,'tp'=2] {'zh'}, dimensions={0} | all-to-all | bytes 147456 | tf_op jit(solution)/shard_map/all_to_all | solution.py:472
  242.8 1.1 merge_far.1
  243.9 9.2 %all-to-all-start.2 = ((bf16[32,8,1024]{2,1,0:T(8,128)(2,1)}), bf16[32,8,1024]{2,1,0:T(8,128)(2,1)S(1)}, u32[]{:S(2)}, u32[]{:S(2)}) async-start(bf16[32,8,1024]{2,1,0:T(8,128)(2,1)} %bitcast.17), calls=%async_computation.2 | async-start | bytes 1048576 | tf_op jit(solution)/shard_map/all_to_all | solution.py:481
  253.2 12.8 %all-to-all-done.2 = bf16[32,8,1024]{2,1,0:T(8,128)(2,1)S(1)} async-done(((bf16[32,8,1024]{2,1,0:T(8,128)(2,1)}), bf16[32,8,1024]{2,1,0:T(8,128)(2,1)S(1)}, u32[]{:S(2)}, u32[]{:S(2)}) %all-to-all-start.2) | async-done | bytes 524320 | tf_op jit(solution)/shard_map/all_to_all | solution.py:481
  266.1 0.8 output_rows.1
  266.9 8.1 %all_to_all.21 = f32[2,64,128]{2,1,0:T(8,128)S(1)} all-to-all(f32[2,64,128]{2,1,0:T(8,128)S(1)} %bitcast.47), channel_id=1, replica_groups=mesh['group'=2,'x'=8,'zh'=4,'zm'=2,'zp'=2,'tp'=2] {'tp'}, dimensions={0} | all-to-all | bytes 131072 | tf_op jit(solution)/shard_map/all_to_all | solution.py:495
  275.0 0.6 reduce_sum.59
  (77 shorter events, 1.7 us)
Async XLA Ops:
  0.0 212.8 %copy-start = (bf16[1,256]{1,0:T(2,128)(2,1)S(1)}, bf16[1,256]{1,0:T(2,128)(2,1)}, u32[]{:S(2)}) copy-start(bf16[1,256]{1,0:T(2,128)(2,1)} %param.27) | copy-start | bytes 1540
  0.0 14.1 %copy-start.15 = (bf16[1,2048]{1,0:T(2,128)(2,1)S(1)}, bf16[1,2048]{1,0:T(2,128)(2,1)}, u32[]{:S(2)}) copy-start(bf16[1,2048]{1,0:T(2,128)(2,1)} %param.26) | copy-start | bytes 12292
  0.0 14.1 %copy-start.11 = (bf16[64,256]{1,0:T(8,128)(2,1)S(1)}, bf16[64,256]{1,0:T(8,128)(2,1)}, u32[]{:S(2)}) copy-start(bf16[64,256]{1,0:T(8,128)(2,1)} %param.19) | copy-start | bytes 98308
  0.0 14.1 %copy-start.12 = (bf16[64,256]{1,0:T(8,128)(2,1)S(1)}, bf16[64,256]{1,0:T(8,128)(2,1)}, u32[]{:S(2)}) copy-start(bf16[64,256]{1,0:T(8,128)(2,1)} %param.18) | copy-start | bytes 98308
  0.0 14.1 %copy-start.14 = (bf16[64,128]{1,0:T(8,128)(2,1)S(1)}, bf16[64,128]{1,0:T(8,128)(2,1)}, u32[]{:S(2)}) copy-start(bf16[64,128]{1,0:T(8,128)(2,1)} %param.20) | copy-start | bytes 49156
  7.4 132.3 %copy-start.10 = (s32[8192,1]{0,1:T(1,128)S(1)}, s32[8192,1]{0,1:T(1,128)}, u32[]{:S(2)}) copy-start(s32[8192,1]{0,1:T(1,128)} %param.24) | copy-start | bytes 98308
  7.4 146.0 %copy-start.7 = (s32[128]{0:T(128)S(1)}, s32[128]{0:T(128)}, u32[]{:S(2)}) copy-start(s32[128]{0:T(128)} %param.23) | copy-start | bytes 1540
  7.4 146.0 %copy-start.17 = (s32[128]{0:T(128)S(1)}, s32[128]{0:T(128)}, u32[]{:S(2)}) copy-start(s32[128]{0:T(128)} %param.25) | copy-start | bytes 1540
  7.4 170.2 %collective-permute-start.14 = (bf16[256,4096]{1,0:T(8,128)(2,1)}, bf16[256,4096]{1,0:T(8,128)(2,1)}, u32[]{:S(2)}, u32[]{:S(2)}) collective-permute-start(bf16[256,4096]{1,0:T(8,128)(2,1)} %get-tuple-element.8), channel_id=1, source_target_pairs={{0,2},{2,0},{1,3},{3,1},{4,6},{6,4},{5,7},{7,5},{8,10},{10,8},{9,1... | collective-permute-start | bytes 6291464 | tf_op jit(solution)/shard_map/ppermute | solution.py:44
  119.0 14.1 %collective-permute-start = (bf16[272,640]{1,0:T(8,128)(2,1)S(1)}, bf16[272,640]{1,0:T(8,128)(2,1)S(1)}, u32[]{:S(2)}, u32[]{:S(2)}) collective-permute-start(bf16[272,640]{1,0:T(8,128)(2,1)S(1)} %pad_maximum_fusion.refs_0_), channel_id=1, source_target_pairs={{0,32},{32,64},{64,96},{96,128},{128,160},{160,192},{192,224},{224... | collective-permute-start | bytes 1044488 | tf_op jit(solution)/shard_map/ppermute | solution.py:40
  122.4 12.7 %collective-permute-start.3 = (bf16[272,640]{1,0:T(8,128)(2,1)S(1)}, bf16[272,640]{1,0:T(8,128)(2,1)S(1)}, u32[]{:S(2)}, u32[]{:S(2)}) collective-permute-start(bf16[272,640]{1,0:T(8,128)(2,1)S(1)} %pad_maximum_fusion.1.refs_1_), channel_id=1, source_target_pairs={{0,224},{32,0},{64,32},{96,64},{128,96},{160,128},{192,160},{224,1... | collective-permute-start | bytes 1044488 | tf_op jit(solution)/shard_map/ppermute | solution.py:40
  126.5 13.3 %collective-permute-start.1 = (bf16[272,640]{1,0:T(8,128)(2,1)S(1)}, bf16[272,640]{1,0:T(8,128)(2,1)S(1)}, u32[]{:S(2)}, u32[]{:S(2)}) collective-permute-start(bf16[272,640]{1,0:T(8,128)(2,1)S(1)} %pad_maximum_fusion.1.refs_1_), channel_id=1, source_target_pairs={{0,32},{32,64},{64,96},{96,128},{128,160},{160,192},{192,224},{224... | collective-permute-start | bytes 1044488 | tf_op jit(solution)/shard_map/ppermute | solution.py:40
  128.5 13.3 %collective-permute-start.2 = (bf16[272,640]{1,0:T(8,128)(2,1)S(1)}, bf16[272,640]{1,0:T(8,128)(2,1)S(1)}, u32[]{:S(2)}, u32[]{:S(2)}) collective-permute-start(bf16[272,640]{1,0:T(8,128)(2,1)S(1)} %pad_maximum_fusion.refs_0_), channel_id=1, source_target_pairs={{0,224},{32,0},{64,32},{96,64},{128,96},{160,128},{192,160},{224,1... | collective-permute-start | bytes 1044488 | tf_op jit(solution)/shard_map/ppermute | solution.py:40
  133.1 13.7 %collective-permute-start.4 = (bf16[272,640]{1,0:T(8,128)(2,1)S(1)}, bf16[272,640]{1,0:T(8,128)(2,1)S(1)}, u32[]{:S(2)}, u32[]{:S(2)}) collective-permute-start(bf16[272,640]{1,0:T(8,128)(2,1)S(1)} %collective-permute-done.refs_2_.refs_14_), channel_id=1, source_target_pairs={{0,32},{32,64},{64,96},{96,128},{128,160},{160,192},{192,224},{224... | collective-permute-start | bytes 1044488 | tf_op jit(solution)/shard_map/ppermute | solution.py:40
  135.1 13.7 %collective-permute-start.7 = (bf16[272,640]{1,0:T(8,128)(2,1)S(1)}, bf16[272,640]{1,0:T(8,128)(2,1)S(1)}, u32[]{:S(2)}, u32[]{:S(2)}) collective-permute-start(bf16[272,640]{1,0:T(8,128)(2,1)S(1)} %collective-permute-done.3.refs_5_.refs_3_), channel_id=1, source_target_pairs={{0,224},{32,0},{64,32},{96,64},{128,96},{160,128},{192,160},{224,1... | collective-permute-start | bytes 1044488 | tf_op jit(solution)/shard_map/ppermute | solution.py:40
  139.8 14.4 %collective-permute-start.5 = (bf16[272,640]{1,0:T(8,128)(2,1)S(1)}, bf16[272,640]{1,0:T(8,128)(2,1)S(1)}, u32[]{:S(2)}, u32[]{:S(2)}) collective-permute-start(bf16[272,640]{1,0:T(8,128)(2,1)S(1)} %collective-permute-done.1.refs_3_.refs_15_), channel_id=1, source_target_pairs={{0,32},{32,64},{64,96},{96,128},{128,160},{160,192},{192,224},{224... | collective-permute-start | bytes 1044488 | tf_op jit(solution)/shard_map/ppermute | solution.py:40
  141.8 14.4 %collective-permute-start.6 = (bf16[272,640]{1,0:T(8,128)(2,1)S(1)}, bf16[272,640]{1,0:T(8,128)(2,1)S(1)}, u32[]{:S(2)}, u32[]{:S(2)}) collective-permute-start(bf16[272,640]{1,0:T(8,128)(2,1)S(1)} %collective-permute-done.2.refs_4_.refs_2_), channel_id=1, source_target_pairs={{0,224},{32,0},{64,32},{96,64},{128,96},{160,128},{192,160},{224,1... | collective-permute-start | bytes 1044488 | tf_op jit(solution)/shard_map/ppermute | solution.py:40
  146.8 14.9 %collective-permute-start.8 = (bf16[272,640]{1,0:T(8,128)(2,1)S(1)}, bf16[272,640]{1,0:T(8,128)(2,1)}, u32[]{:S(2)}, u32[]{:S(2)}) collective-permute-start(bf16[272,640]{1,0:T(8,128)(2,1)S(1)} %collective-permute-done.4.refs_6_.refs_12_), channel_id=1, source_target_pairs={{0,32},{32,64},{64,96},{96,128},{128,160},{160,192},{192,224},{224... | collective-permute-start | bytes 1044488 | tf_op jit(solution)/shard_map/ppermute | solution.py:40
  148.7 14.9 %collective-permute-start.11 = (bf16[272,640]{1,0:T(8,128)(2,1)S(1)}, bf16[272,640]{1,0:T(8,128)(2,1)}, u32[]{:S(2)}, u32[]{:S(2)}) collective-permute-start(bf16[272,640]{1,0:T(8,128)(2,1)S(1)} %collective-permute-done.7.refs_9_.refs_5_), channel_id=1, source_target_pairs={{0,224},{32,0},{64,32},{96,64},{128,96},{160,128},{192,160},{224,1... | collective-permute-start | bytes 1044488 | tf_op jit(solution)/shard_map/ppermute | solution.py:40
  154.2 15.0 %collective-permute-start.9 = (bf16[272,640]{1,0:T(8,128)(2,1)S(1)}, bf16[272,640]{1,0:T(8,128)(2,1)}, u32[]{:S(2)}, u32[]{:S(2)}) collective-permute-start(bf16[272,640]{1,0:T(8,128)(2,1)S(1)} %collective-permute-done.5.refs_7_.refs_13_), channel_id=1, source_target_pairs={{0,32},{32,64},{64,96},{96,128},{128,160},{160,192},{192,224},{224... | collective-permute-start | bytes 1044488 | tf_op jit(solution)/shard_map/ppermute | solution.py:40
  156.2 13.8 %collective-permute-start.10 = (bf16[272,640]{1,0:T(8,128)(2,1)S(1)}, bf16[272,640]{1,0:T(8,128)(2,1)}, u32[]{:S(2)}, u32[]{:S(2)}) collective-permute-start(bf16[272,640]{1,0:T(8,128)(2,1)S(1)} %collective-permute-done.6.refs_8_.refs_4_), channel_id=1, source_target_pairs={{0,224},{32,0},{64,32},{96,64},{128,96},{160,128},{192,160},{224,1... | collective-permute-start | bytes 1044488 | tf_op jit(solution)/shard_map/ppermute | solution.py:40
  161.7 15.0 %collective-permute-start.12 = (bf16[272,640]{1,0:T(8,128)(2,1)}, bf16[272,640]{1,0:T(8,128)(2,1)}, u32[]{:S(2)}, u32[]{:S(2)}) collective-permute-start(bf16[272,640]{1,0:T(8,128)(2,1)} %collective-permute-done.8.refs_10_), channel_id=1, source_target_pairs={{0,32},{32,64},{64,96},{96,128},{128,160},{160,192},{192,224},{224... | collective-permute-start | bytes 1044488 | tf_op jit(solution)/shard_map/ppermute | solution.py:40
  163.7 13.9 %collective-permute-start.13 = (bf16[272,640]{1,0:T(8,128)(2,1)}, bf16[272,640]{1,0:T(8,128)(2,1)}, u32[]{:S(2)}, u32[]{:S(2)}) collective-permute-start(bf16[272,640]{1,0:T(8,128)(2,1)} %collective-permute-done.11.refs_13_.refs_7_), channel_id=1, source_target_pairs={{0,224},{32,0},{64,32},{96,64},{128,96},{160,128},{192,160},{224,1... | collective-permute-start | bytes 1044488 | tf_op jit(solution)/shard_map/ppermute | solution.py:40
  182.3 15.5 %collective-permute-start.15 = (bf16[256,640]{1,0:T(8,128)(2,1)}, bf16[256,640]{1,0:T(8,128)(2,1)}, u32[]{:S(2)}, u32[]{:S(2)}) collective-permute-start(bf16[256,640]{1,0:T(8,128)(2,1)} %project.3.after_ref), channel_id=1, source_target_pairs={{0,2},{2,0},{1,3},{3,1},{4,6},{6,4},{5,7},{7,5},{8,10},{10,8},{9,1... | collective-permute-start | bytes 983048 | tf_op jit(solution)/shard_map/ppermute | solution.py:44
  185.8 12.0 %collective-permute-start.16 = (bf16[256,512]{1,0:T(8,128)(2,1)}, bf16[256,512]{1,0:T(8,128)(2,1)}, u32[]{:S(2)}, u32[]{:S(2)}) collective-permute-start(bf16[256,512]{1,0:T(8,128)(2,1)} %collect_tails.1.q0_ref), channel_id=1, source_target_pairs={{0,2},{2,0},{1,3},{3,1},{4,6},{6,4},{5,7},{7,5},{8,10},{10,8},{9,1... | collective-permute-start | bytes 786440 | tf_op jit(solution)/shard_map/ppermute | solution.py:44
  192.8 1.6 copy-start.1
  194.4 3.4 %copy-start.2 = (s32[256,1]{1,0:T(8,128)S(1)}, s32[256,1]{1,0:T(8,128)}, u32[]{:S(2)}) copy-start(s32[256,1]{1,0:T(8,128)} %reshape.132.adapter_ref) | copy-start | bytes 3076
  194.4 3.4 %copy-start.5 = (bf16[64,256]{1,0:T(8,128)(2,1)S(1)}, bf16[64,256]{1,0:T(8,128)(2,1)}, u32[]{:S(2)}) copy-start(bf16[64,256]{1,0:T(8,128)(2,1)} %upk_ref.1) | copy-start | bytes 98308
  194.4 3.4 %copy-start.6 = (bf16[64,256]{1,0:T(8,128)(2,1)S(1)}, bf16[64,256]{1,0:T(8,128)(2,1)}, u32[]{:S(2)}) copy-start(bf16[64,256]{1,0:T(8,128)(2,1)} %upv_ref.1) | copy-start | bytes 98308
  197.8 13.7 %copy-start.8 = (bf16[1,256,256]{2,1,0:T(8,128)(2,1)S(1)}, bf16[1,256,256]{2,1,0:T(8,128)(2,1)}, u32[]{:S(2)}) copy-start(bf16[1,256,256]{2,1,0:T(8,128)(2,1)} %param.30) | copy-start | bytes 393220
  197.8 13.7 %copy-start.9 = (bf16[1,256,256]{2,1,0:T(8,128)(2,1)S(1)}, bf16[1,256,256]{2,1,0:T(8,128)(2,1)}, u32[]{:S(2)}) copy-start(bf16[1,256,256]{2,1,0:T(8,128)(2,1)} %param.29) | copy-start | bytes 393220
  197.9 13.7 %copy-start.16 = (bf16[1,256]{1,0:T(2,128)(2,1)S(1)}, bf16[1,256]{1,0:T(2,128)(2,1)}, u32[]{:S(2)}) copy-start(bf16[1,256]{1,0:T(2,128)(2,1)} %param.28) | copy-start | bytes 1540
  202.9 50.2 %copy-start.13 = (bf16[64,64]{1,0:T(8,128)(2,1)S(1)}, bf16[64,64]{1,0:T(8,128)(2,1)}, u32[]{:S(2)}) copy-start(bf16[64,64]{1,0:T(8,128)(2,1)} %param.33) | copy-start | bytes 24580
  202.9 63.2 %copy-start.3 = (bf16[2048,64]{0,1:T(8,128)(2,1)S(1)}, bf16[2048,64]{0,1:T(8,128)(2,1)}, u32[]{:S(2)}) copy-start(bf16[2048,64]{0,1:T(8,128)(2,1)} %param.31) | copy-start | bytes 786436
  202.9 63.2 %copy-start.4 = (bf16[2048,64]{0,1:T(8,128)(2,1)S(1)}, bf16[2048,64]{0,1:T(8,128)(2,1)}, u32[]{:S(2)}) copy-start(bf16[2048,64]{0,1:T(8,128)(2,1)} %param.32) | copy-start | bytes 786436
  202.9 21.4 %all-to-all-start = ((bf16[32,8,1152]{2,1,0:T(8,128)(2,1)}), bf16[32,8,1152]{2,1,0:T(8,128)(2,1)S(1)}, u32[]{:S(2)}, u32[]{:S(2)}) async-start(bf16[32,8,1152]{2,1,0:T(8,128)(2,1)} %bitcast.9), calls=%async_computation | async-start | bytes 1179648 | tf_op jit(solution)/shard_map/all_to_all | solution.py:463
  243.9 22.1 %all-to-all-start.2 = ((bf16[32,8,1024]{2,1,0:T(8,128)(2,1)}), bf16[32,8,1024]{2,1,0:T(8,128)(2,1)S(1)}, u32[]{:S(2)}, u32[]{:S(2)}) async-start(bf16[32,8,1024]{2,1,0:T(8,128)(2,1)} %bitcast.17), calls=%async_computation.2 | async-start | bytes 1048576 | tf_op jit(solution)/shard_map/all_to_all | solution.py:481

commit v3 on v2

--- a/solution.py
+++ b/solution.py
@@ -44,38 +44,35 @@
     return lax.ppermute(x, "zp", [(0, 1), (1, 0)])
 
 
-def split_kernel(p_ref, a_ref, mine_ref, other_ref):
+def select_kernel(p_ref, a_ref, out_ref):
     half = HEAD // 2
 
-    def write(even_ref, odd_ref):
-        for k in range(even_ref.shape[1] // HEAD):
-            t0 = a_ref[:, 2 * k * HEAD : (2 * k + 1) * HEAD]
-            t1 = a_ref[:, (2 * k + 1) * HEAD : (2 * k + 2) * HEAD]
-            cols = slice(k * HEAD, (k + 1) * HEAD)
-            even_ref[:, cols] = jnp.concatenate([t0[:, :half], t1[:, :half]], axis=1)
-            odd_ref[:, cols] = jnp.concatenate([t0[:, half:], t1[:, half:]], axis=1)
+    def write(at):
+        for k in range(out_ref.shape[1] // HEAD):
+            t0 = a_ref[:, 2 * k * HEAD + at : 2 * k * HEAD + at + half]
+            t1 = a_ref[:, (2 * k + 1) * HEAD + at : (2 * k + 1) * HEAD + at + half]
+            out_ref[:, k * HEAD : (k + 1) * HEAD] = jnp.concatenate([t0, t1], axis=1)
 
     @pl.when(p_ref[0] == 0)
     def _():
-        write(mine_ref, other_ref)
+        write(0)
 
     @pl.when(p_ref[0] != 0)
     def _():
-        write(other_ref, mine_ref)
-
-
-def split_columns(act, parity):
+        write(half)
+
+
+def select_columns(act, parity, mib):
     rows, width = act.shape
     block = 32
-    out = jax.ShapeDtypeStruct((rows, width // 2), bf16)
     return pl.pallas_call(
-        split_kernel,
+        select_kernel,
         grid=(rows // block,),
         in_specs=[SMEM, pl.BlockSpec((block, width), lambda i: (i, 0))],
-        out_specs=[pl.BlockSpec((block, width // 2), lambda i: (i, 0))] * 2,
-        out_shape=[out, out],
-        compiler_params=room(58),
-        name="split_columns",
+        out_specs=pl.BlockSpec((block, width // 2), lambda i: (i, 0)),
+        out_shape=jax.ShapeDtypeStruct((rows, width // 2), bf16),
+        compiler_params=room(mib),
+        name="select_columns",
     )(parity, act)
 
 
@@ -386,7 +383,8 @@
         )
     chunk_depth = per_chunk * depth
 
-    mine, theirs = split_columns(prompt_activations, parity[None])
+    theirs = select_columns(prompt_activations, 1 - parity[None], 58)
+    mine = select_columns(prompt_activations, parity[None], 50)
     partner_act = swap_pair(theirs)
 
     by_offset = {0: pieces}

time: 277 us -> 286 us (1.032)
  blocking collectives: 131 us -> 139 us
  starting transfers between devices: 76.5 us -> 70.7 us
  local copies, waits for them, and re-layouts: 3.06 us -> 7.36 us
  Pallas kernels: 24.5 us -> 28.6 us
    all_to_all x1, blocking collectives: 8.11 us -> 17.6 us  [per_device(): lax.all_to_all(partial_output.reshape(pair, columns, requests), 'tp', 0,...]
    all_to_all x1, starting transfers between devices: 9.2 us -> 4.8 us  [per_device(): lax.all_to_all(mixed.reshape(members, unit, half_width), NEAR, 0, 0, tile...]
    unnamed x38 -> x60, local copies, waits for them, and re-layouts: 1.75 us -> 6.07 us
    pallas_call x1 -> x2, Pallas kernels: 7.35 us -> 11.6 us  [select_columns(): pl.pallas_call(select_kernel, grid=(rows // block,), in_specs=[SMEM, pl.B...]
  transfers between devices with their start and end apart: 19 -> 19, of which waited for: 8 -> 8; matrix products, arithmetic and copies ran while one was open for 3% -> 3% of each run, Pallas kernels for 2% -> 3%
where the time goes in v3:
time: 286 us; the launch traced here: 285 us
  blocking collectives  139 us (49%)
  starting transfers between devices  70.7 us (25%)
  waiting for transfers between devices  32.3 us (11%)
  Pallas kernels  28.6 us (10%)
  local copies, waits for them, and re-layouts  7.36 us (3%)
  other arithmetic  5.81 us (2%)
    all_gather x1, blocking collectives, per_device(): column = lax.all_gather(block, Z8)  105 us
    ppermute x14, starting transfers between devices, ring_x(): return lax.ppermute(x, 'x', [(i, (i + step) % NX) for i in range(NX)])  44.8 us
    all_to_all x1, blocking collectives, per_device(): lax.all_to_all(partial_output.reshape(pair, columns, requests), 'tp', 0,...  17.6 us
    all_to_all x1, blocking collectives, per_device(): lax.all_to_all(merged.reshape(NZH, unit, full_width), 'zh', 0, 0, tiled=T...  16.6 us
    ppermute x3, starting transfers between devices, swap_pair(): return lax.ppermute(x, 'zp', [(0, 1), (1, 0)])  12 us
    all_to_all x1, waiting for transfers between devices, per_device(): lax.all_to_all(mixed.reshape(members, unit, half_width), NEAR, 0, 0, tile...  12 us
    pallas_call x2, Pallas kernels, select_columns(): pl.pallas_call(select_kernel, grid=(rows // block,), in_specs=[SMEM, pl.B...  11.6 us
    all_to_all x1, waiting for transfers between devices, per_device(): lax.all_to_all(payload.reshape(members, unit, full_width), NEAR, 0, 0, ti...  10.3 us
  transfers between devices with their start and end apart: 19, of which 8 were waited for; matrix products, arithmetic and copies ran while one was open for 3% of the time, Pallas kernels for 3%

profile of v3, /device:TPU:65, one launch (start us, length us, event | category | flops | bytes accessed | tf_op | source)
XLA Modules:
  0.0 284.9 jit_solution(9455281381825475438)
XLA Ops:
  0.0 6.5 %select_columns.3 = bf16[256,4096]{1,0:T(8,128)(2,1)} custom-call(s32[1]{0:T(128)S(6)} %sub.25.p_ref, bf16[256,8192]{1,0:T(8,128)(2,1)} %a_ref.3), custom_call_target="tpu_custom_call" | custom-call | tf_op jit(solution)/shard_map/select_columns/pallas_call | solution.py:68
  6.6 6.7 %collective-permute-start.14 = (bf16[256,4096]{1,0:T(8,128)(2,1)}, bf16[256,4096]{1,0:T(8,128)(2,1)}, u32[]{:S(2)}, u32[]{:S(2)}) collective-permute-start(bf16[256,4096]{1,0:T(8,128)(2,1)} %select_columns.3), channel_id=1, source_target_pairs={{0,2},{2,0},{1,3},{3,1},{4,6},{6,4},{5,7},{7,5},{8,10},{10,8},{9,1... | collective-permute-start | bytes 6291464 | tf_op jit(solution)/shard_map/ppermute | solution.py:44
  13.4 104.7 %all-gather = bf16[576,640]{1,0:T(8,128)(2,1)S(1)} all-gather(bf16[72,640]{1,0:T(8,128)(2,1)S(1)} %fusion.6), channel_id=2, replica_groups=mesh['group'=2,'x'=8,'zh'=4,'zm'=2,'zp'=2,'tp'=2] {'zh','zm'}, dimensions={0}, use_global_device_ids=true | all-gather | bytes 829440 | tf_op jit(solution)/shard_map/all_gather | solution.py:368
  118.2 3.3 %collective-permute-start = (bf16[272,640]{1,0:T(8,128)(2,1)S(1)}, bf16[272,640]{1,0:T(8,128)(2,1)S(1)}, u32[]{:S(2)}, u32[]{:S(2)}) collective-permute-start(bf16[272,640]{1,0:T(8,128)(2,1)S(1)} %pad_maximum_fusion.refs_0_), channel_id=1, source_target_pairs={{0,32},{32,64},{64,96},{96,128},{128,160},{160,192},{192,224},{224... | collective-permute-start | bytes 1044488 | tf_op jit(solution)/shard_map/ppermute | solution.py:40
  121.6 4.1 %collective-permute-start.3 = (bf16[272,640]{1,0:T(8,128)(2,1)S(1)}, bf16[272,640]{1,0:T(8,128)(2,1)S(1)}, u32[]{:S(2)}, u32[]{:S(2)}) collective-permute-start(bf16[272,640]{1,0:T(8,128)(2,1)S(1)} %pad_maximum_fusion.1.refs_1_), channel_id=1, source_target_pairs={{0,224},{32,0},{64,32},{96,64},{128,96},{160,128},{192,160},{224,1... | collective-permute-start | bytes 1044488 | tf_op jit(solution)/shard_map/ppermute | solution.py:40
  125.7 3.4 %collective-permute-start.2 = (bf16[272,640]{1,0:T(8,128)(2,1)S(1)}, bf16[272,640]{1,0:T(8,128)(2,1)S(1)}, u32[]{:S(2)}, u32[]{:S(2)}) collective-permute-start(bf16[272,640]{1,0:T(8,128)(2,1)S(1)} %pad_maximum_fusion.refs_0_), channel_id=1, source_target_pairs={{0,224},{32,0},{64,32},{96,64},{128,96},{160,128},{192,160},{224,1... | collective-permute-start | bytes 1044488 | tf_op jit(solution)/shard_map/ppermute | solution.py:40
  129.1 2.0 collective-permute-start.1
  131.1 2.0 collective-permute-start.4
  133.1 4.6 %collective-permute-start.7 = (bf16[272,640]{1,0:T(8,128)(2,1)S(1)}, bf16[272,640]{1,0:T(8,128)(2,1)S(1)}, u32[]{:S(2)}, u32[]{:S(2)}) collective-permute-start(bf16[272,640]{1,0:T(8,128)(2,1)S(1)} %collective-permute-done.3.refs_5_.refs_3_), channel_id=1, source_target_pairs={{0,224},{32,0},{64,32},{96,64},{128,96},{160,128},{192,160},{224,1... | collective-permute-start | bytes 1044488 | tf_op jit(solution)/shard_map/ppermute | solution.py:40
  137.8 3.4 %collective-permute-start.6 = (bf16[272,640]{1,0:T(8,128)(2,1)S(1)}, bf16[272,640]{1,0:T(8,128)(2,1)S(1)}, u32[]{:S(2)}, u32[]{:S(2)}) collective-permute-start(bf16[272,640]{1,0:T(8,128)(2,1)S(1)} %collective-permute-done.2.refs_4_.refs_2_), channel_id=1, source_target_pairs={{0,224},{32,0},{64,32},{96,64},{128,96},{160,128},{192,160},{224,1... | collective-permute-start | bytes 1044488 | tf_op jit(solution)/shard_map/ppermute | solution.py:40
  141.3 2.0 collective-permute-start.5
  143.3 3.2 %collective-permute-start.8 = (bf16[272,640]{1,0:T(8,128)(2,1)S(1)}, bf16[272,640]{1,0:T(8,128)(2,1)}, u32[]{:S(2)}, u32[]{:S(2)}) collective-permute-start(bf16[272,640]{1,0:T(8,128)(2,1)S(1)} %collective-permute-done.4.refs_6_.refs_12_), channel_id=1, source_target_pairs={{0,32},{32,64},{64,96},{96,128},{128,160},{160,192},{192,224},{224... | collective-permute-start | bytes 1044488 | tf_op jit(solution)/shard_map/ppermute | solution.py:40
  146.6 4.3 %collective-permute-start.11 = (bf16[272,640]{1,0:T(8,128)(2,1)S(1)}, bf16[272,640]{1,0:T(8,128)(2,1)}, u32[]{:S(2)}, u32[]{:S(2)}) collective-permute-start(bf16[272,640]{1,0:T(8,128)(2,1)S(1)} %collective-permute-done.7.refs_9_.refs_5_), channel_id=1, source_target_pairs={{0,224},{32,0},{64,32},{96,64},{128,96},{160,128},{192,160},{224,1... | collective-permute-start | bytes 1044488 | tf_op jit(solution)/shard_map/ppermute | solution.py:40
  151.1 0.6 convert_reduce_fusion
  152.1 4.1 %collective-permute-start.10 = (bf16[272,640]{1,0:T(8,128)(2,1)S(1)}, bf16[272,640]{1,0:T(8,128)(2,1)}, u32[]{:S(2)}, u32[]{:S(2)}) collective-permute-start(bf16[272,640]{1,0:T(8,128)(2,1)S(1)} %collective-permute-done.6.refs_8_.refs_4_), channel_id=1, source_target_pairs={{0,224},{32,0},{64,32},{96,64},{128,96},{160,128},{192,160},{224,1... | collective-permute-start | bytes 1044488 | tf_op jit(solution)/shard_map/ppermute | solution.py:40
  156.2 2.0 collective-permute-start.9
  158.2 1.4 collective-permute-done.8.refs_10_
  159.6 2.5 collective-permute-start.12
  162.1 4.1 %collective-permute-start.13 = (bf16[272,640]{1,0:T(8,128)(2,1)}, bf16[272,640]{1,0:T(8,128)(2,1)}, u32[]{:S(2)}, u32[]{:S(2)}) collective-permute-start(bf16[272,640]{1,0:T(8,128)(2,1)} %collective-permute-done.11.refs_13_.refs_7_), channel_id=1, source_target_pairs={{0,224},{32,0},{64,32},{96,64},{128,96},{160,128},{192,160},{224,1... | collective-permute-start | bytes 1044488 | tf_op jit(solution)/shard_map/ppermute | solution.py:40
  166.4 3.0 %collective-permute-done.9.refs_11_ = bf16[272,640]{1,0:T(8,128)(2,1)} collective-permute-done((bf16[272,640]{1,0:T(8,128)(2,1)S(1)}, bf16[272,640]{1,0:T(8,128)(2,1)}, u32[]{:S(2)}, u32[]{:S(2)}) %collective-permute-start.9) | collective-permute-done | bytes 348192 | tf_op jit(solution)/shard_map/ppermute | solution.py:40
  169.3 3.6 %collective-permute-done.12.refs_14_.refs_8_ = bf16[272,640]{1,0:T(8,128)(2,1)} collective-permute-done((bf16[272,640]{1,0:T(8,128)(2,1)}, bf16[272,640]{1,0:T(8,128)(2,1)}, u32[]{:S(2)}, u32[]{:S(2)}) %collective-permute-start.12) | collective-permute-done | bytes 348192 | tf_op jit(solution)/shard_map/ppermute | solution.py:40
  172.9 1.5 collective-permute-done.13.refs_15_.refs_9_
  174.4 4.7 %project.3.after_ref = bf16[256,640]{1,0:T(8,128)(2,1)} custom-call(s32[1]{0:T(128)} %bitcast.1.x_ref, bf16[256,4096]{1,0:T(8,128)(2,1)} %collective-permute-done.14.a_ref, bf16[272,640]{1,0:T(8,128)(2,1)S(1)} %pad_maximum_fusion.refs_0_, bf16[272,640]{1,0:T(8,128)(2,1)S(1)} %pad_maximum_fusion.1.refs_1_, ...), custom_call_target="tpu_custom_call" | custom-call | tf_op jit(solution)/shard_map/project/pallas_call | solution.py:98
  179.1 1.9 collective-permute-start.15
  181.1 1.6 collect_tails.1.q0_ref
  182.7 3.4 %collective-permute-start.16 = (bf16[256,512]{1,0:T(8,128)(2,1)}, bf16[256,512]{1,0:T(8,128)(2,1)}, u32[]{:S(2)}, u32[]{:S(2)}) collective-permute-start(bf16[256,512]{1,0:T(8,128)(2,1)} %collect_tails.1.q0_ref), channel_id=1, source_target_pairs={{0,2},{2,0},{1,3},{3,1},{4,6},{6,4},{5,7},{7,5},{8,10},{10,8},{9,1... | collective-permute-start | bytes 786440 | tf_op jit(solution)/shard_map/ppermute | solution.py:44
  186.1 1.3 fusion.7
  187.4 5.1 %select_columns.2.a_ref = bf16[256,4096]{1,0:T(8,128)(2,1)S(1)} custom-call(s32[1]{0:T(128)} %bitcast.2.p_ref, bf16[256,8192]{1,0:T(8,128)(2,1)} %a_ref.3), custom_call_target="tpu_custom_call" | custom-call | tf_op jit(solution)/shard_map/select_columns/pallas_call | solution.py:68
  192.5 0.7 reshape.132.adapter_ref
  193.5 1.2 pad_maximum_fusion.2
  194.8 1.0 copy-done.2
  195.7 1.0 copy-done.4
  196.7 1.0 copy-done.6
  197.7 1.0 copy-done.8
  198.7 1.0 copy-done.10
  199.7 1.0 copy-done.12
  200.6 3.4 %project.2.base_ref = f32[256,640]{1,0:T(8,128)S(1)} custom-call(s32[1]{0:T(128)} %bitcast.1.x_ref, bf16[256,4096]{1,0:T(8,128)(2,1)S(1)} %select_columns.2.a_ref, bf16[272,640]{1,0:T(8,128)(2,1)S(1)} %pad_maximum_fusion.refs_0_, bf16[272,640]{1,0:T(8,128)(2,1)S(1)} %pad_maximum_fusion.1.refs_1_, bf16[272,640]{1,0:T(8,128)(2,1)S(1)} %collective-permute-done.refs_2_.refs_14_, ...), custom_call_target="tpu_custom_call" | custom-call | tf_op jit(solution)/shard_map/project/pallas_call | solution.py:98
  204.1 5.0 %partial_attention.1 = bf16[256,1152]{1,0:T(8,128)(2,1)} custom-call(s32[2]{0:T(128)S(1)} %pad_add_fusion.s_ref, f32[256,640]{1,0:T(8,128)S(1)} %project.2.base_ref, bf16[256,640]{1,0:T(8,128)(2,1)} %collective-permute-done.15.other_ref, bf16[64,256]{1,0:T(8,128)(2,1)S(1)} %copy-done.16, bf16[64,256]{1,0:T(8,128)(2,1)S(1)} %copy-done.17, ...), custom_call_target="tpu_custom_call" | custom-call | tf_op jit(solution)/shard_map/partial_attention/pallas_call | solution.py:450
  209.1 9.0 %all-to-all-start = ((bf16[32,8,1152]{2,1,0:T(8,128)(2,1)}), bf16[32,8,1152]{2,1,0:T(8,128)(2,1)S(1)}, u32[]{:S(2)}, u32[]{:S(2)}) async-start(bf16[32,8,1152]{2,1,0:T(8,128)(2,1)} %bitcast.9), calls=%async_computation | async-start | bytes 1179648 | tf_op jit(solution)/shard_map/all_to_all | solution.py:461
  218.2 0.7 fusion.16
  218.9 0.6 iota_compare_fusion.3
  220.3 10.3 %all-to-all-done = bf16[32,8,1152]{2,1,0:T(8,128)(2,1)S(1)} async-done(((bf16[32,8,1152]{2,1,0:T(8,128)(2,1)}), bf16[32,8,1152]{2,1,0:T(8,128)(2,1)S(1)}, u32[]{:S(2)}, u32[]{:S(2)}) %all-to-all-start) | async-done | bytes 589856 | tf_op jit(solution)/shard_map/all_to_all | solution.py:461
  231.2 16.6 %all_to_all.20 = bf16[4,8,1152]{2,1,0:T(8,128)(2,1)S(1)} all-to-all(bf16[4,8,1152]{2,1,0:T(8,128)(2,1)S(1)} %bitcast.45), channel_id=1, replica_groups=mesh['group'=2,'x'=8,'zh'=4,'zm'=2,'zp'=2,'tp'=2] {'zh'}, dimensions={0} | all-to-all | bytes 147456 | tf_op jit(solution)/shard_map/all_to_all | solution.py:470
  247.7 1.1 merge_far.1
  248.9 4.8 %all-to-all-start.2 = ((bf16[32,8,1024]{2,1,0:T(8,128)(2,1)}), bf16[32,8,1024]{2,1,0:T(8,128)(2,1)S(1)}, u32[]{:S(2)}, u32[]{:S(2)}) async-start(bf16[32,8,1024]{2,1,0:T(8,128)(2,1)} %bitcast.17), calls=%async_computation.2 | async-start | bytes 1048576 | tf_op jit(solution)/shard_map/all_to_all | solution.py:479
  253.8 12.0 %all-to-all-done.2 = bf16[32,8,1024]{2,1,0:T(8,128)(2,1)S(1)} async-done(((bf16[32,8,1024]{2,1,0:T(8,128)(2,1)}), bf16[32,8,1024]{2,1,0:T(8,128)(2,1)S(1)}, u32[]{:S(2)}, u32[]{:S(2)}) %all-to-all-start.2) | async-done | bytes 524320 | tf_op jit(solution)/shard_map/all_to_all | solution.py:479
  265.8 0.8 output_rows.1
  266.6 17.6 %all_to_all.21 = f32[2,64,128]{2,1,0:T(8,128)S(1)} all-to-all(f32[2,64,128]{2,1,0:T(8,128)S(1)} %bitcast.47), channel_id=1, replica_groups=mesh['group'=2,'x'=8,'zh'=4,'zm'=2,'zp'=2,'tp'=2] {'tp'}, dimensions={0} | all-to-all | bytes 131072 | tf_op jit(solution)/shard_map/all_to_all | solution.py:493
  (100 shorter events, 3.7 us)
Async XLA Ops:
  0.0 219.5 %copy-start = (bf16[1,256]{1,0:T(2,128)(2,1)S(1)}, bf16[1,256]{1,0:T(2,128)(2,1)}, u32[]{:S(2)}) copy-start(bf16[1,256]{1,0:T(2,128)(2,1)} %param.27) | copy-start | bytes 1540
  0.0 13.3 %copy-start.26 = (bf16[1,2048]{1,0:T(2,128)(2,1)S(1)}, bf16[1,2048]{1,0:T(2,128)(2,1)}, u32[]{:S(2)}) copy-start(bf16[1,2048]{1,0:T(2,128)(2,1)} %param.26) | copy-start | bytes 12292
  0.0 13.4 %copy-start.22 = (bf16[64,256]{1,0:T(8,128)(2,1)S(1)}, bf16[64,256]{1,0:T(8,128)(2,1)}, u32[]{:S(2)}) copy-start(bf16[64,256]{1,0:T(8,128)(2,1)} %param.19) | copy-start | bytes 98308
  0.0 13.4 %copy-start.23 = (bf16[64,256]{1,0:T(8,128)(2,1)S(1)}, bf16[64,256]{1,0:T(8,128)(2,1)}, u32[]{:S(2)}) copy-start(bf16[64,256]{1,0:T(8,128)(2,1)} %param.18) | copy-start | bytes 98308
  0.0 13.4 %copy-start.25 = (bf16[64,128]{1,0:T(8,128)(2,1)S(1)}, bf16[64,128]{1,0:T(8,128)(2,1)}, u32[]{:S(2)}) copy-start(bf16[64,128]{1,0:T(8,128)(2,1)} %param.20) | copy-start | bytes 49156
  6.6 131.1 %copy-start.21 = (s32[8192,1]{0,1:T(1,128)S(1)}, s32[8192,1]{0,1:T(1,128)}, u32[]{:S(2)}) copy-start(s32[8192,1]{0,1:T(1,128)} %param.24) | copy-start | bytes 98308
  6.6 144.3 %copy-start.18 = (s32[128]{0:T(128)S(1)}, s32[128]{0:T(128)}, u32[]{:S(2)}) copy-start(s32[128]{0:T(128)} %param.23) | copy-start | bytes 1540
  6.6 144.3 %copy-start.28 = (s32[128]{0:T(128)S(1)}, s32[128]{0:T(128)}, u32[]{:S(2)}) copy-start(s32[128]{0:T(128)} %param.25) | copy-start | bytes 1540
  6.6 167.9 %collective-permute-start.14 = (bf16[256,4096]{1,0:T(8,128)(2,1)}, bf16[256,4096]{1,0:T(8,128)(2,1)}, u32[]{:S(2)}, u32[]{:S(2)}) collective-permute-start(bf16[256,4096]{1,0:T(8,128)(2,1)} %select_columns.3), channel_id=1, source_target_pairs={{0,2},{2,0},{1,3},{3,1},{4,6},{6,4},{5,7},{7,5},{8,10},{10,8},{9,1... | collective-permute-start | bytes 6291464 | tf_op jit(solution)/shard_map/ppermute | solution.py:44
  118.2 12.9 %collective-permute-start = (bf16[272,640]{1,0:T(8,128)(2,1)S(1)}, bf16[272,640]{1,0:T(8,128)(2,1)S(1)}, u32[]{:S(2)}, u32[]{:S(2)}) collective-permute-start(bf16[272,640]{1,0:T(8,128)(2,1)S(1)} %pad_maximum_fusion.refs_0_), channel_id=1, source_target_pairs={{0,32},{32,64},{64,96},{96,128},{128,160},{160,192},{192,224},{224... | collective-permute-start | bytes 1044488 | tf_op jit(solution)/shard_map/ppermute | solution.py:40
  121.6 11.5 %collective-permute-start.3 = (bf16[272,640]{1,0:T(8,128)(2,1)S(1)}, bf16[272,640]{1,0:T(8,128)(2,1)S(1)}, u32[]{:S(2)}, u32[]{:S(2)}) collective-permute-start(bf16[272,640]{1,0:T(8,128)(2,1)S(1)} %pad_maximum_fusion.1.refs_1_), channel_id=1, source_target_pairs={{0,224},{32,0},{64,32},{96,64},{128,96},{160,128},{192,160},{224,1... | collective-permute-start | bytes 1044488 | tf_op jit(solution)/shard_map/ppermute | solution.py:40
  125.7 12.1 %collective-permute-start.2 = (bf16[272,640]{1,0:T(8,128)(2,1)S(1)}, bf16[272,640]{1,0:T(8,128)(2,1)S(1)}, u32[]{:S(2)}, u32[]{:S(2)}) collective-permute-start(bf16[272,640]{1,0:T(8,128)(2,1)S(1)} %pad_maximum_fusion.refs_0_), channel_id=1, source_target_pairs={{0,224},{32,0},{64,32},{96,64},{128,96},{160,128},{192,160},{224,1... | collective-permute-start | bytes 1044488 | tf_op jit(solution)/shard_map/ppermute | solution.py:40
  129.1 12.1 %collective-permute-start.1 = (bf16[272,640]{1,0:T(8,128)(2,1)S(1)}, bf16[272,640]{1,0:T(8,128)(2,1)S(1)}, u32[]{:S(2)}, u32[]{:S(2)}) collective-permute-start(bf16[272,640]{1,0:T(8,128)(2,1)S(1)} %pad_maximum_fusion.1.refs_1_), channel_id=1, source_target_pairs={{0,32},{32,64},{64,96},{96,128},{128,160},{160,192},{192,224},{224... | collective-permute-start | bytes 1044488 | tf_op jit(solution)/shard_map/ppermute | solution.py:40
  131.1 12.2 %collective-permute-start.4 = (bf16[272,640]{1,0:T(8,128)(2,1)S(1)}, bf16[272,640]{1,0:T(8,128)(2,1)S(1)}, u32[]{:S(2)}, u32[]{:S(2)}) collective-permute-start(bf16[272,640]{1,0:T(8,128)(2,1)S(1)} %collective-permute-done.refs_2_.refs_14_), channel_id=1, source_target_pairs={{0,32},{32,64},{64,96},{96,128},{128,160},{160,192},{192,224},{224... | collective-permute-start | bytes 1044488 | tf_op jit(solution)/shard_map/ppermute | solution.py:40
  133.1 13.5 %collective-permute-start.7 = (bf16[272,640]{1,0:T(8,128)(2,1)S(1)}, bf16[272,640]{1,0:T(8,128)(2,1)S(1)}, u32[]{:S(2)}, u32[]{:S(2)}) collective-permute-start(bf16[272,640]{1,0:T(8,128)(2,1)S(1)} %collective-permute-done.3.refs_5_.refs_3_), channel_id=1, source_target_pairs={{0,224},{32,0},{64,32},{96,64},{128,96},{160,128},{192,160},{224,1... | collective-permute-start | bytes 1044488 | tf_op jit(solution)/shard_map/ppermute | solution.py:40
  137.8 43.3 %copy-start.1 = (bf16[272,640]{1,0:T(8,128)(2,1)}, bf16[272,640]{1,0:T(8,128)(2,1)S(1)}, u32[]{:S(2)}) copy-start(bf16[272,640]{1,0:T(8,128)(2,1)S(1)} %collective-permute-done.2.refs_4_.refs_2_) | copy-start | bytes 1044484
  137.8 14.3 %collective-permute-start.6 = (bf16[272,640]{1,0:T(8,128)(2,1)S(1)}, bf16[272,640]{1,0:T(8,128)(2,1)S(1)}, u32[]{:S(2)}, u32[]{:S(2)}) collective-permute-start(bf16[272,640]{1,0:T(8,128)(2,1)S(1)} %collective-permute-done.2.refs_4_.refs_2_), channel_id=1, source_target_pairs={{0,224},{32,0},{64,32},{96,64},{128,96},{160,128},{192,160},{224,1... | collective-permute-start | bytes 1044488 | tf_op jit(solution)/shard_map/ppermute | solution.py:40
  141.2 39.8 %copy-start.3 = (bf16[272,640]{1,0:T(8,128)(2,1)}, bf16[272,640]{1,0:T(8,128)(2,1)S(1)}, u32[]{:S(2)}) copy-start(bf16[272,640]{1,0:T(8,128)(2,1)S(1)} %collective-permute-done.1.refs_3_.refs_15_) | copy-start | bytes 1044484
  141.3 15.0 %collective-permute-start.5 = (bf16[272,640]{1,0:T(8,128)(2,1)S(1)}, bf16[272,640]{1,0:T(8,128)(2,1)S(1)}, u32[]{:S(2)}, u32[]{:S(2)}) collective-permute-start(bf16[272,640]{1,0:T(8,128)(2,1)S(1)} %collective-permute-done.1.refs_3_.refs_15_), channel_id=1, source_target_pairs={{0,32},{32,64},{64,96},{96,128},{128,160},{160,192},{192,224},{224... | collective-permute-start | bytes 1044488 | tf_op jit(solution)/shard_map/ppermute | solution.py:40
  143.3 37.8 %copy-start.5 = (bf16[272,640]{1,0:T(8,128)(2,1)}, bf16[272,640]{1,0:T(8,128)(2,1)S(1)}, u32[]{:S(2)}) copy-start(bf16[272,640]{1,0:T(8,128)(2,1)S(1)} %collective-permute-done.4.refs_6_.refs_12_) | copy-start | bytes 1044484
  143.3 16.3 %collective-permute-start.8 = (bf16[272,640]{1,0:T(8,128)(2,1)S(1)}, bf16[272,640]{1,0:T(8,128)(2,1)}, u32[]{:S(2)}, u32[]{:S(2)}) collective-permute-start(bf16[272,640]{1,0:T(8,128)(2,1)S(1)} %collective-permute-done.4.refs_6_.refs_12_), channel_id=1, source_target_pairs={{0,32},{32,64},{64,96},{96,128},{128,160},{160,192},{192,224},{224... | collective-permute-start | bytes 1044488 | tf_op jit(solution)/shard_map/ppermute | solution.py:40
  146.6 34.5 %copy-start.7 = (bf16[272,640]{1,0:T(8,128)(2,1)}, bf16[272,640]{1,0:T(8,128)(2,1)S(1)}, u32[]{:S(2)}) copy-start(bf16[272,640]{1,0:T(8,128)(2,1)S(1)} %collective-permute-done.7.refs_9_.refs_5_) | copy-start | bytes 1044484
  146.6 15.5 %collective-permute-start.11 = (bf16[272,640]{1,0:T(8,128)(2,1)S(1)}, bf16[272,640]{1,0:T(8,128)(2,1)}, u32[]{:S(2)}, u32[]{:S(2)}) collective-permute-start(bf16[272,640]{1,0:T(8,128)(2,1)S(1)} %collective-permute-done.7.refs_9_.refs_5_), channel_id=1, source_target_pairs={{0,224},{32,0},{64,32},{96,64},{128,96},{160,128},{192,160},{224,1... | collective-permute-start | bytes 1044488 | tf_op jit(solution)/shard_map/ppermute | solution.py:40
  152.1 29.0 %copy-start.9 = (bf16[272,640]{1,0:T(8,128)(2,1)}, bf16[272,640]{1,0:T(8,128)(2,1)S(1)}, u32[]{:S(2)}) copy-start(bf16[272,640]{1,0:T(8,128)(2,1)S(1)} %collective-permute-done.6.refs_8_.refs_4_) | copy-start | bytes 1044484
  152.1 14.2 %collective-permute-start.10 = (bf16[272,640]{1,0:T(8,128)(2,1)S(1)}, bf16[272,640]{1,0:T(8,128)(2,1)}, u32[]{:S(2)}, u32[]{:S(2)}) collective-permute-start(bf16[272,640]{1,0:T(8,128)(2,1)S(1)} %collective-permute-done.6.refs_8_.refs_4_), channel_id=1, source_target_pairs={{0,224},{32,0},{64,32},{96,64},{128,96},{160,128},{192,160},{224,1... | collective-permute-start | bytes 1044488 | tf_op jit(solution)/shard_map/ppermute | solution.py:40
  156.2 24.9 %copy-start.11 = (bf16[272,640]{1,0:T(8,128)(2,1)}, bf16[272,640]{1,0:T(8,128)(2,1)S(1)}, u32[]{:S(2)}) copy-start(bf16[272,640]{1,0:T(8,128)(2,1)S(1)} %collective-permute-done.5.refs_7_.refs_13_) | copy-start | bytes 1044484
  156.2 13.1 %collective-permute-start.9 = (bf16[272,640]{1,0:T(8,128)(2,1)S(1)}, bf16[272,640]{1,0:T(8,128)(2,1)}, u32[]{:S(2)}, u32[]{:S(2)}) collective-permute-start(bf16[272,640]{1,0:T(8,128)(2,1)S(1)} %collective-permute-done.5.refs_7_.refs_13_), channel_id=1, source_target_pairs={{0,32},{32,64},{64,96},{96,128},{128,160},{160,192},{192,224},{224... | collective-permute-start | bytes 1044488 | tf_op jit(solution)/shard_map/ppermute | solution.py:40
  159.6 13.4 %collective-permute-start.12 = (bf16[272,640]{1,0:T(8,128)(2,1)}, bf16[272,640]{1,0:T(8,128)(2,1)}, u32[]{:S(2)}, u32[]{:S(2)}) collective-permute-start(bf16[272,640]{1,0:T(8,128)(2,1)} %collective-permute-done.8.refs_10_), channel_id=1, source_target_pairs={{0,32},{32,64},{64,96},{96,128},{128,160},{160,192},{192,224},{224... | collective-permute-start | bytes 1044488 | tf_op jit(solution)/shard_map/ppermute | solution.py:40
  162.1 12.4 %collective-permute-start.13 = (bf16[272,640]{1,0:T(8,128)(2,1)}, bf16[272,640]{1,0:T(8,128)(2,1)}, u32[]{:S(2)}, u32[]{:S(2)}) collective-permute-start(bf16[272,640]{1,0:T(8,128)(2,1)} %collective-permute-done.11.refs_13_.refs_7_), channel_id=1, source_target_pairs={{0,224},{32,0},{64,32},{96,64},{128,96},{160,128},{192,160},{224,1... | collective-permute-start | bytes 1044488 | tf_op jit(solution)/shard_map/ppermute | solution.py:40
  179.1 24.9 %collective-permute-start.15 = (bf16[256,640]{1,0:T(8,128)(2,1)}, bf16[256,640]{1,0:T(8,128)(2,1)}, u32[]{:S(2)}, u32[]{:S(2)}) collective-permute-start(bf16[256,640]{1,0:T(8,128)(2,1)} %project.3.after_ref), channel_id=1, source_target_pairs={{0,2},{2,0},{1,3},{3,1},{4,6},{6,4},{5,7},{7,5},{8,10},{10,8},{9,1... | collective-permute-start | bytes 983048 | tf_op jit(solution)/shard_map/ppermute | solution.py:44
  182.7 21.3 %collective-permute-start.16 = (bf16[256,512]{1,0:T(8,128)(2,1)}, bf16[256,512]{1,0:T(8,128)(2,1)}, u32[]{:S(2)}, u32[]{:S(2)}) collective-permute-start(bf16[256,512]{1,0:T(8,128)(2,1)} %collect_tails.1.q0_ref), channel_id=1, source_target_pairs={{0,2},{2,0},{1,3},{3,1},{4,6},{6,4},{5,7},{7,5},{8,10},{10,8},{9,1... | collective-permute-start | bytes 786440 | tf_op jit(solution)/shard_map/ppermute | solution.py:44
  194.8 1.0 copy-start.2
  195.7 1.0 copy-start.4
  196.7 1.0 copy-start.6
  197.7 1.0 copy-start.8
  198.7 1.0 copy-start.10
  199.7 1.0 copy-start.12
  200.6 3.4 %copy-start.13 = (s32[256,1]{1,0:T(8,128)S(1)}, s32[256,1]{1,0:T(8,128)}, u32[]{:S(2)}) copy-start(s32[256,1]{1,0:T(8,128)} %reshape.132.adapter_ref) | copy-start | bytes 3076
  200.6 3.4 %copy-start.16 = (bf16[64,256]{1,0:T(8,128)(2,1)S(1)}, bf16[64,256]{1,0:T(8,128)(2,1)}, u32[]{:S(2)}) copy-start(bf16[64,256]{1,0:T(8,128)(2,1)} %upk_ref.1) | copy-start | bytes 98308
  200.6 3.4 %copy-start.17 = (bf16[64,256]{1,0:T(8,128)(2,1)S(1)}, bf16[64,256]{1,0:T(8,128)(2,1)}, u32[]{:S(2)}) copy-start(bf16[64,256]{1,0:T(8,128)(2,1)} %upv_ref.1) | copy-start | bytes 98308
  204.0 14.1 %copy-start.19 = (bf16[1,256,256]{2,1,0:T(8,128)(2,1)S(1)}, bf16[1,256,256]{2,1,0:T(8,128)(2,1)}, u32[]{:S(2)}) copy-start(bf16[1,256,256]{2,1,0:T(8,128)(2,1)} %param.29) | copy-start | bytes 393220
  204.0 14.2 %copy-start.20 = (bf16[1,256,256]{2,1,0:T(8,128)(2,1)S(1)}, bf16[1,256,256]{2,1,0:T(8,128)(2,1)}, u32[]{:S(2)}) copy-start(bf16[1,256,256]{2,1,0:T(8,128)(2,1)} %param.30) | copy-start | bytes 393220
  204.1 14.1 %copy-start.27 = (bf16[1,256]{1,0:T(2,128)(2,1)S(1)}, bf16[1,256]{1,0:T(2,128)(2,1)}, u32[]{:S(2)}) copy-start(bf16[1,256]{1,0:T(2,128)(2,1)} %param.28) | copy-start | bytes 1540
  209.1 44.6 %copy-start.24 = (bf16[64,64]{1,0:T(8,128)(2,1)S(1)}, bf16[64,64]{1,0:T(8,128)(2,1)}, u32[]{:S(2)}) copy-start(bf16[64,64]{1,0:T(8,128)(2,1)} %param.33) | copy-start | bytes 24580
  209.1 56.7 %copy-start.14 = (bf16[2048,64]{0,1:T(8,128)(2,1)S(1)}, bf16[2048,64]{0,1:T(8,128)(2,1)}, u32[]{:S(2)}) copy-start(bf16[2048,64]{0,1:T(8,128)(2,1)} %param.31) | copy-start | bytes 786436
  209.1 56.7 %copy-start.15 = (bf16[2048,64]{0,1:T(8,128)(2,1)S(1)}, bf16[2048,64]{0,1:T(8,128)(2,1)}, u32[]{:S(2)}) copy-start(bf16[2048,64]{0,1:T(8,128)(2,1)} %param.32) | copy-start | bytes 786436
  209.1 21.5 %all-to-all-start = ((bf16[32,8,1152]{2,1,0:T(8,128)(2,1)}), bf16[32,8,1152]{2,1,0:T(8,128)(2,1)S(1)}, u32[]{:S(2)}, u32[]{:S(2)}) async-start(bf16[32,8,1152]{2,1,0:T(8,128)(2,1)} %bitcast.9), calls=%async_computation | async-start | bytes 1179648 | tf_op jit(solution)/shard_map/all_to_all | solution.py:461
  248.9 16.9 %all-to-all-start.2 = ((bf16[32,8,1024]{2,1,0:T(8,128)(2,1)}), bf16[32,8,1024]{2,1,0:T(8,128)(2,1)S(1)}, u32[]{:S(2)}, u32[]{:S(2)}) async-start(bf16[32,8,1024]{2,1,0:T(8,128)(2,1)} %bitcast.17), calls=%async_computation.2 | async-start | bytes 1048576 | tf_op jit(solution)/shard_map/all_to_all | solution.py:479
